TPU v7x, 32 devices: a whole 2x2x4 slice. The times are simulated.
32 devices in a mesh: sx: 4 (over y, x), sy: 8 (over z, core).
Axes of the slice: x: 2, y: 2, z: 4, core: 2. Of those that a mesh axis runs over, the one named last changes fastest.
Arguments:
- collocation: float32 [2, 4, 2048], P(None, 'sx', 'sy'), may hold values from -1 to 1
- source: float32 [4, 2048], P('sx', 'sy'), may hold values from -31.5 to 40.5
- wall_index: int32 [4, 4, 512], P(None, 'sx', 'sy'), may hold values from 0 to 1023, as said below
- bc_type: int32 [2, 8], P(None, 'sy'), may hold values from 0 to 1
- bc_value: float32 [2, 512], P(None, 'sy'), may hold values from -4 to 4
- in_weight: float32 [4, 3, 4096], P('sx', None, 'sy'), may hold values from -4 to 4
- local_weight: bfloat16 [4, 512, 4096], P('sx', None, 'sy'), may hold values from -0.25 to 0.25
- local_bias: float32 [4, 4096], P('sx', 'sy'), may hold values from -3 to 3
- trunk_weight: bfloat16 [1, 512, 512], replicated, may hold values from -0.25 to 0.25
- trunk_bias: float32 [1, 512], replicated, may hold values from -3 to 3
- head_weight: float32 [4, 4096], P('sx', 'sy'), may hold values from -0.25 to 0.25
Outputs:
- trunk_grad: float32 [1, 512, 512], replicated
- trunk_bias_grad: float32 [1, 512], replicated
- in_grad: float32 [4, 3, 4096], P('sx', None, 'sy')
- local_grad: float32 [4, 512, 4096], P('sx', None, 'sy')
- local_bias_grad: float32 [4, 4096], P('sx', 'sy')
- head_grad: float32 [4, 4096], P('sx', 'sy')
- loss_value: float32 [], replicated
Inputs may be any that keep to these rules, and one draw needn't show every extreme that they name: `wall_index`: within a wall the positions are distinct. A shared wall has the same positions on both sides: wall 0 of (i, j) equals wall 1 of (i - 1, j), and wall 2 of (i, j) equals wall 3 of (i, (j - 1) mod 8).
All inputs are finite; a program needn't handle non-finite values.
Results may differ from a plain program's by a relative error of at most 0.0016.
Values sent between devices are 32-bit elements; how exact they have to be, the bound alone decides.
No kernel may reach another device: no remote copies, remote signals or barrier semaphores. Data moves between devices by JAX's collectives and lax.ppermute only.
A program may use at most 64 MiB of HBM per device.

v0:
```python
import functools

import jax
import jax.numpy as jnp
from jax import lax
from jax.experimental import pallas as pl
from jax.experimental.pallas import tpu as pltpu
from jax.sharding import PartitionSpec as P


SLOTS = 1024
EPS = 1e-06
TILE = 16
LANES = 128
F32 = jnp.float32
BF16 = jnp.bfloat16


def nn(a, b):
    return lax.dot_general(a, b, (((1,), (0,)), ((), ())), preferred_element_type=F32)


def nt(a, b):
    return lax.dot_general(a, b, (((1,), (1,)), ((), ())), preferred_element_type=F32)


def tn(a, b):
    return lax.dot_general(a, b, (((0,), (0,)), ((), ())), preferred_element_type=F32)


def eye_mask(rows, cols, shift=0):
    r = lax.broadcasted_iota(jnp.int32, (rows, cols), 0)
    c = lax.broadcasted_iota(jnp.int32, (rows, cols), 1)
    return r + shift == c


def to_column(row):
    size = row.shape[1]
    return jnp.sum(jnp.where(eye_mask(size, size), row, 0.0), axis=1, keepdims=True)


def chunks(width):
    return [slice(k, k + LANES) for k in range(0, width, LANES)]


def fold(parts):
    return [jnp.sum(p, axis=0, keepdims=True) for p in parts]


def zeros_tile():
    return jnp.zeros((TILE, LANES), F32)


def rows_of(i):
    return pl.ds(pl.multiple_of(i * TILE, TILE), TILE)


def wall_columns(index_ref, s_ref, t_ref):
    edge = index_ref.shape[2]
    shape = (edge, LANES)
    for w in range(4):
        spots = (2.0 * index_ref[w].astype(F32) + 1.0) / SLOTS - 1.0
        moving = jnp.broadcast_to(to_column(spots), shape)
        fixed = jnp.full(shape, -1.0 if w % 2 == 0 else 1.0, F32)
        where = pl.ds(w * edge, edge)
        s_ref[where, :] = fixed if w < 2 else moving
        t_ref[where, :] = moving if w < 2 else fixed


def wall_forward_kernel(*refs):
    far, refs = refs[:7], refs[7:]
    (rims_ref, s_ref, t_ref, a0_ref, x0_ref, z1_ref, x1_ref, z2_ref), refs = refs[:8], refs[8:]
    ua_ref, da_ref, sems = refs[:3]
    near = refs[3:]
    copies = [pltpu.make_async_copy(f, n, sems.at[k]) for k, (f, n) in enumerate(zip(far, near))]
    index_ref, win_ref, wl_ref, bl_ref, wt_ref, bt_ref, head_ref = near
    for copy in copies:
        copy.start()
    edge = index_ref.shape[2]
    points, width = a0_ref.shape
    copies[0].wait()
    copies[1].wait()
    wall_columns(index_ref, s_ref, t_ref)

    for direction in range(2):
        def entry(i, carry, direction=direction):
            rows = rows_of(i)
            s, t = s_ref[rows, :], t_ref[rows, :]
            for c in chunks(width):
                w0, w1, wb = (win_ref[k, :, c] for k in range(3))
                a = jnp.tanh(s * w0 + t * w1 + wb)
                slope = 1.0 - a * a
                a0_ref[rows, c] = a
                x0_ref[0, rows, c] = a.astype(BF16)
                x0_ref[1, rows, c] = (slope * (2.0 * (w0, w1)[direction])).astype(BF16)
            return carry

        tiles = points // (2 * TILE)
        lax.fori_loop(direction * tiles, (direction + 1) * tiles, entry, 0, unroll=2)

    for copy in copies[2:]:
        copy.wait()
    z1_ref[...] = nn(x0_ref[...].reshape(2 * points, width), wl_ref[0]).reshape(2, points, width)

    def hidden(i, carry):
        rows = rows_of(i)
        for c in chunks(width):
            a = jnp.tanh(z1_ref[0, rows, c] + bl_ref[:, c])
            slope = 1.0 - a * a
            z1_ref[0, rows, c] = a
            x1_ref[0, rows, c] = a.astype(BF16)
            x1_ref[1, rows, c] = (slope * z1_ref[1, rows, c]).astype(BF16)
        return carry

    lax.fori_loop(0, points // TILE, hidden, 0, unroll=2)
    z2_ref[...] = nn(x1_ref[...].reshape(2 * points, width), wt_ref[0]).reshape(2, points, width)

    def final(i, carry):
        rows = rows_of(i)
        u, d = zeros_tile(), zeros_tile()
        for c in chunks(width):
            a = jnp.tanh(z2_ref[0, rows, c] + bt_ref[:, c])
            slope = 1.0 - a * a
            z2_ref[0, rows, c] = a
            u += a * head_ref[:, c]
            d += slope * z2_ref[1, rows, c] * head_ref[:, c]
        ua_ref[rows, :] = u
        da_ref[rows, :] = d
        return carry

    lax.fori_loop(0, points // TILE, final, 0, unroll=2)
    value = jnp.sum(ua_ref[...], axis=1, keepdims=True)
    slope = jnp.sum(da_ref[...], axis=1, keepdims=True)
    low, high = eye_mask(edge, 2 * edge), eye_mask(edge, 2 * edge, edge)
    for w in range(4):
        part = slice(w * edge, (w + 1) * edge)
        both = jnp.where(low, value[part], 0.0) + jnp.where(high, slope[part], 0.0)
        rims_ref[w : w + 1, :] = jnp.sum(both, axis=0, keepdims=True)


def inner_kernel(
    order_size, order_of,
    points_ref, source_ref, win_ref, wl_ref, bl_ref, wt_ref, bt_ref, head_ref,
    grad_ref, sums_ref, s_ref, t_ref, a0_ref, x0_ref, z1_ref, g2_ref,
    x1_ref, z2_ref, acc_ref,
):
    points, width = a0_ref.shape
    for k in range(0, points, LANES):
        where = pl.ds(k, LANES)
        for ref, which in ((s_ref, 0), (t_ref, 1)):
            column = to_column(points_ref[which, :, k : k + LANES])
            ref[where, :] = jnp.broadcast_to(column, (LANES, LANES))

    def entry(i, carry):
        rows = rows_of(i)
        s, t = s_ref[rows, :], t_ref[rows, :]
        for c in chunks(width):
            w0, w1, wb = (win_ref[k, :, c] for k in range(3))
            p0, p1 = 2.0 * w0, 2.0 * w1
            a = jnp.tanh(s * w0 + t * w1 + wb)
            slope = 1.0 - a * a
            bend = -2.0 * a * slope
            a0_ref[rows, c] = a
            x0_ref[0, rows, c] = a.astype(BF16)
            x0_ref[1, rows, c] = (slope * p0).astype(BF16)
            x0_ref[2, rows, c] = (slope * p1).astype(BF16)
            x0_ref[3, rows, c] = (bend * (p0 * p0)).astype(BF16)
            x0_ref[4, rows, c] = (bend * (p1 * p1)).astype(BF16)
        return carry

    tiles = points // TILE
    lax.fori_loop(0, tiles, entry, 0, unroll=2)
    z1_ref[...] = nn(x0_ref[...].reshape(5 * points, width), wl_ref[0]).reshape(5, points, width)

    def hidden(i, carry):
        rows = rows_of(i)
        for c in chunks(width):
            a = jnp.tanh(z1_ref[0, rows, c] + bl_ref[:, c])
            p0, p1 = z1_ref[1, rows, c], z1_ref[2, rows, c]
            slope = 1.0 - a * a
            bend = -2.0 * a * slope
            z1_ref[0, rows, c] = a
            x1_ref[0, rows, c] = a.astype(BF16)
            x1_ref[1, rows, c] = (slope * p0).astype(BF16)
            x1_ref[2, rows, c] = (slope * p1).astype(BF16)
            x1_ref[3, rows, c] = (slope * z1_ref[3, rows, c] + bend * p0 * p0).astype(BF16)
            x1_ref[4, rows, c] = (slope * z1_ref[4, rows, c] + bend * p1 * p1).astype(BF16)
        return carry

    lax.fori_loop(0, tiles, hidden, 0, unroll=2)
    z2_ref[...] = nn(x1_ref[...].reshape(5 * points, width), wt_ref[0]).reshape(5, points, width)

    def final(i, carry):
        rows = rows_of(i)
        total = zeros_tile()
        for c in chunks(width):
            a = jnp.tanh(z2_ref[0, rows, c] + bt_ref[:, c])
            p0, p1 = z2_ref[1, rows, c], z2_ref[2, rows, c]
            slope = 1.0 - a * a
            bend = -2.0 * a * slope
            second = z2_ref[3, rows, c] + z2_ref[4, rows, c]
            bent = slope * second + bend * (p0 * p0 + p1 * p1)
            z2_ref[0, rows, c] = a
            z2_ref[3, rows, c] = second
            z2_ref[4, rows, c] = bent
            total += bent * head_ref[:, c]
        acc_ref[rows, :] = total
        return carry

    lax.fori_loop(0, tiles, final, 0, unroll=2)
    residual = jnp.sum(acc_ref[...], axis=1, keepdims=True)
    forcing = [to_column(source_ref[:, k : k + LANES]) for k in range(0, points, LANES)]
    residual = residual + jnp.concatenate(forcing, axis=0)
    acc_ref[...] = jnp.broadcast_to(2.0 * residual, acc_ref.shape)
    square = jnp.sum(residual * residual, axis=0, keepdims=True)

    spans = chunks(width)

    def top(i, carry):
        rows = rows_of(i)
        heads, biases = list(carry[0]), list(carry[1])
        twice = acc_ref[rows, :]
        for n, c in enumerate(spans):
            a = z2_ref[0, rows, c]
            p0, p1 = z2_ref[1, rows, c], z2_ref[2, rows, c]
            slope = 1.0 - a * a
            bend = -2.0 * a * slope
            g = twice * head_ref[:, c]
            heads[n] += twice * z2_ref[4, rows, c]
            gc = g * (p0 * p0 + p1 * p1)
            gs = g * z2_ref[3, rows, c] - 2.0 * a * gc
            g0 = slope * (-2.0 * (gc * slope + gs * a))
            bg = 2.0 * bend * g
            g3 = (slope * g).astype(BF16)
            biases[n] += g0
            g2_ref[0, rows, c] = g0.astype(BF16)
            g2_ref[1, rows, c] = (bg * p0).astype(BF16)
            g2_ref[2, rows, c] = (bg * p1).astype(BF16)
            g2_ref[3, rows, c] = g3
            g2_ref[4, rows, c] = g3
        return tuple(heads), tuple(biases)

    blank = tuple(zeros_tile() for _ in spans)
    heads, biases = lax.fori_loop(0, tiles, top, (blank, blank))
    sums_ref[...] = jnp.zeros(sums_ref.shape, F32)
    for c, hp, bp in zip(spans, fold(heads), fold(biases)):
        sums_ref[0:1, c] = bp
        sums_ref[1:2, c] = hp
    sums_ref[2:3, :] = jnp.broadcast_to(square, (1, width))
    store_ordered(
        grad_ref,
        tn(x1_ref[...].reshape(5 * points, width), g2_ref[...].reshape(5 * points, width)),
        order_size, order_of,
    )


def store_ordered(grad_ref, grad, order_size, order_of):
    mine = order_of()
    size = grad.shape[0] // order_size
    for block in range(order_size):
        where = pl.ds(pl.multiple_of((mine ^ block) * size, size), size)
        grad_ref[where, :] = grad[block * size : (block + 1) * size]


def wall_top_kernel(
    order_size, order_of, row_size,
    rims_ref, west_ref, east_ref, south_ref, north_ref, type_ref, value_ref,
    z2_ref, x1_ref, head_ref, isums_ref,
    grad_ref, sums_ref, heads_ref, g2_ref,
    cu_ref, cd_ref,
):
    _, points, width = z2_ref.shape
    edge = points // 4
    place = lax.axis_index("sx")
    outer = (place == 0, place == row_size - 1)
    low, high = eye_mask(edge, 2 * edge), eye_mask(edge, 2 * edge, edge)
    total = jnp.zeros((1, 1), F32)

    def split(row):
        u = jnp.sum(jnp.where(low, row, 0.0), axis=1, keepdims=True)
        d = jnp.sum(jnp.where(high, row, 0.0), axis=1, keepdims=True)
        return u, d

    for w, near in enumerate((west_ref, east_ref, south_ref, north_ref)):
        u, d = split(rims_ref[w : w + 1, :])
        un, dn = split(near[...])
        eu, ed = u - un, d - dn
        if w < 2:
            normal = -1.0 if w == 0 else 1.0
            g = to_column(value_ref[w : w + 1, :])
            fixed = type_ref[:, w : w + 1] == 0
            bu = jnp.where(fixed, u - g, 0.0)
            bd = jnp.where(fixed, 0.0, normal * (normal * d - g))
            eu = jnp.where(outer[w], bu, eu)
            ed = jnp.where(outer[w], bd, ed)
        total += jnp.sum(eu * eu + ed * ed, axis=0, keepdims=True)
        where = pl.ds(w * edge, edge)
        cu_ref[where, :] = jnp.broadcast_to(2.0 * eu, (edge, LANES))
        cd_ref[where, :] = jnp.broadcast_to(2.0 * ed, (edge, LANES))

    spans = chunks(width)

    def top(i, carry):
        rows = rows_of(i)
        heads, biases = list(carry[0]), list(carry[1])
        cu, cd = cu_ref[rows, :], cd_ref[rows, :]
        for n, c in enumerate(spans):
            a, p = z2_ref[0, rows, c], z2_ref[1, rows, c]
            slope = 1.0 - a * a
            h = head_ref[:, c]
            gv, gd = cu * h, cd * h
            heads[n] += cu * a + cd * (slope * p)
            g0 = slope * (gv - 2.0 * a * (gd * p))
            biases[n] += g0
            g2_ref[0, rows, c] = g0.astype(BF16)
            g2_ref[1, rows, c] = (slope * gd).astype(BF16)
        return tuple(heads), tuple(biases)

    blank = tuple(zeros_tile() for _ in spans)
    heads, biases = lax.fori_loop(0, points // TILE, top, (blank, blank))
    sums_ref[...] = jnp.zeros(sums_ref.shape, F32)
    for c, hp, bp in zip(spans, fold(heads), fold(biases)):
        sums_ref[1:2, c] = bp
        heads_ref[:, c] = hp
    sums_ref[0:1, :] = isums_ref[0:1, :]
    sums_ref[2:3, :] = isums_ref[2:3, :]
    sums_ref[3:4, :] = jnp.broadcast_to(total, (1, width))
    store_ordered(
        grad_ref,
        tn(x1_ref[...].reshape(2 * points, width), g2_ref[...].reshape(2 * points, width)),
        order_size, order_of,
    )


def factors(total_r, total_b, inner_count, wall_count):
    mean_r = total_r / inner_count
    mean_b = total_b / wall_count
    lam = jnp.sqrt((mean_b + EPS) / (mean_r + EPS))
    return lam / inner_count, 1.0 / wall_count, lam * mean_r + mean_b


def unorder_kernel(order_size, order_of, *refs):
    ins, out_ref = refs[:order_size], refs[order_size]
    size = ins[0].shape[0]
    mine = order_of()
    for place, ref in enumerate(ins):
        where = pl.ds(pl.multiple_of((mine ^ place) * size, size), size)
        out_ref[0, where, :] = ref[...]


def back(g_ref, count, weight, u_ref):
    _, size, width = g_ref.shape
    flat = g_ref[0:count].reshape(count * size, width)
    u_ref[...] = nt(flat, weight).reshape(count, size, width)


def hidden_kernel(
    wt_ref, z1i_ref, g2i_ref, z1w_ref, g2w_ref,
    gi_ref, gw_ref, biases_ref,
    ui_ref, uw_ref,
):
    _, points, width = z1i_ref.shape
    rims = z1w_ref.shape[1]
    spans = chunks(width)
    blank = tuple(zeros_tile() for _ in spans)

    back(g2i_ref, 4, wt_ref[0], ui_ref)

    def inner_hidden(i, carry):
        rows = rows_of(i)
        biases = list(carry)
        for n, c in enumerate(spans):
            a, p0, p1 = z1i_ref[0, rows, c], z1i_ref[1, rows, c], z1i_ref[2, rows, c]
            u0, u1, u2, u3 = (ui_ref[k, rows, c] for k in range(4))
            slope = 1.0 - a * a
            bend = -2.0 * a * slope
            gc = u3 * (p0 * p0 + p1 * p1)
            second = z1i_ref[3, rows, c] + z1i_ref[4, rows, c]
            gs = u1 * p0 + u2 * p1 + u3 * second - 2.0 * a * gc
            g0 = slope * (u0 - 2.0 * (gc * slope + gs * a))
            bg = 2.0 * bend * u3
            g3 = (slope * u3).astype(BF16)
            biases[n] += g0
            gi_ref[0, rows, c] = g0.astype(BF16)
            gi_ref[1, rows, c] = (slope * u1 + bg * p0).astype(BF16)
            gi_ref[2, rows, c] = (slope * u2 + bg * p1).astype(BF16)
            gi_ref[3, rows, c] = g3
            gi_ref[4, rows, c] = g3
        return tuple(biases)

    bias_i = lax.fori_loop(0, points // TILE, inner_hidden, blank)
    back(g2w_ref, 2, wt_ref[0], uw_ref)

    def wall_hidden(i, carry):
        rows = rows_of(i)
        biases = list(carry)
        for n, c in enumerate(spans):
            a, p = z1w_ref[0, rows, c], z1w_ref[1, rows, c]
            u0, u1 = uw_ref[0, rows, c], uw_ref[1, rows, c]
            slope = 1.0 - a * a
            g0 = slope * (u0 - 2.0 * a * (u1 * p))
            biases[n] += g0
            gw_ref[0, rows, c] = g0.astype(BF16)
            gw_ref[1, rows, c] = (slope * u1).astype(BF16)
        return tuple(biases)

    bias_w = lax.fori_loop(0, rims // TILE, wall_hidden, blank)
    biases_ref[...] = jnp.zeros(biases_ref.shape, F32)
    for c, bi, bw in zip(spans, fold(bias_i), fold(bias_w)):
        biases_ref[0:1, c] = bi
        biases_ref[1:2, c] = bw


def entry_kernel(
    win_ref, wl_ref,
    si_ref, ti_ref, a0i_ref, gi_ref, sw_ref, tw_ref, a0w_ref, gw_ref, biases_ref,
    parts_ref,
    ui_ref, uw_ref,
):
    points, width = a0i_ref.shape
    rims = a0w_ref.shape[0]
    spans = chunks(width)
    blank = tuple(zeros_tile() for _ in spans)
    back(gi_ref, 4, wl_ref[0], ui_ref)

    def inner_entry(i, carry):
        rows = rows_of(i)
        k0, k1, k2 = (list(part) for part in carry)
        s, t = si_ref[rows, :], ti_ref[rows, :]
        for n, c in enumerate(spans):
            a = a0i_ref[rows, c]
            p0, p1 = 2.0 * win_ref[0, :, c], 2.0 * win_ref[1, :, c]
            u0, u1, u2, u3 = (ui_ref[k, rows, c] for k in range(4))
            slope = 1.0 - a * a
            bend = -2.0 * a * slope
            gc = u3 * (p0 * p0 + p1 * p1)
            gs = u1 * p0 + u2 * p1 - 2.0 * a * gc
            g0 = slope * (u0 - 2.0 * (gc * slope + gs * a))
            bg = 2.0 * bend * u3
            k0[n] += s * g0 + 2.0 * (slope * u1 + bg * p0)
            k1[n] += t * g0 + 2.0 * (slope * u2 + bg * p1)
            k2[n] += g0
        return tuple(k0), tuple(k1), tuple(k2)

    entry_i = lax.fori_loop(0, points // TILE, inner_entry, (blank, blank, blank))
    back(gw_ref, 2, wl_ref[0], uw_ref)
    entry_w = (blank, blank, blank)
    for direction in range(2):
        def wall_entry(i, carry, direction=direction):
            rows = rows_of(i)
            k0, k1, k2 = (list(part) for part in carry)
            s, t = sw_ref[rows, :], tw_ref[rows, :]
            for n, c in enumerate(spans):
                a = a0w_ref[rows, c]
                p = 2.0 * win_ref[direction, :, c]
                u0, u1 = uw_ref[0, rows, c], uw_ref[1, rows, c]
                slope = 1.0 - a * a
                g0 = slope * (u0 - 2.0 * a * (u1 * p))
                along = 2.0 * (slope * u1)
                k0[n] += s * g0 + along if direction == 0 else s * g0
                k1[n] += t * g0 + along if direction == 1 else t * g0
                k2[n] += g0
            return tuple(k0), tuple(k1), tuple(k2)

        tiles = rims // (2 * TILE)
        entry_w = lax.fori_loop(direction * tiles, (direction + 1) * tiles, wall_entry, entry_w)
    parts_ref[3:4, :] = biases_ref[0:1, :]
    parts_ref[7:8, :] = biases_ref[1:2, :]
    for k in range(3):
        for c, ei, ew in zip(spans, fold(entry_i[k]), fold(entry_w[k])):
            parts_ref[k : k + 1, c] = ei
            parts_ref[4 + k : 5 + k, c] = ew


def blend_kernel(
    inner_count, wall_count,
    sums_ref, parts_ref, isums_ref, wheads_ref, x0i_ref, gi_ref, x0w_ref, gw_ref,
    in_ref, local_ref, bias_ref, head_ref, tbias_ref, loss_ref,
):
    count, points, width = x0i_ref.shape
    rims = x0w_ref.shape[1]
    fr, fb, loss = factors(sums_ref[2:3, :], sums_ref[3:4, :], inner_count, wall_count)
    loss_ref[...] = loss[:, 0:1]
    tbias_ref[...] = fr * sums_ref[0:1, :] + fb * sums_ref[1:2, :]
    head_ref[...] = fr * isums_ref[1:2, :] + fb * wheads_ref[...]
    for k in range(3):
        in_ref[k] = fr * parts_ref[k : k + 1, :] + fb * parts_ref[4 + k : 5 + k, :]
    bias_ref[...] = fr * parts_ref[3:4, :] + fb * parts_ref[7:8, :]
    local_ref[0] = fr * tn(
        x0i_ref[...].reshape(count * points, width), gi_ref[...].reshape(count * points, width)
    ) + fb * tn(x0w_ref[...].reshape(2 * rims, width), gw_ref[...].reshape(2 * rims, width))


def call(kernel, outs, scratch, args, flops, space=pltpu.VMEM):
    vmem = pl.BlockSpec(memory_space=pltpu.VMEM)
    return pl.pallas_call(
        kernel,
        out_shape=outs,
        in_specs=[pl.BlockSpec(memory_space=space)] * len(args),
        out_specs=jax.tree.map(lambda _: vmem, outs),
        scratch_shapes=scratch,
        compiler_params=pltpu.CompilerParams(vmem_limit_bytes=20 << 20),
        cost_estimate=pl.CostEstimate(flops=flops, bytes_accessed=0, transcendentals=0),
    )(*args)


def shape(*dims, dtype=F32):
    return jax.ShapeDtypeStruct(dims, dtype)


def swap(x, axis, bit):
    return exchange(x, axis, 1 << bit)


def exchange(x, axis, mask):
    return lax.ppermute(x, axis, [(i, i ^ mask) for i in range(lax.axis_size(axis))])


def bits_of(axis):
    return [(axis, bit) for bit in range(lax.axis_size(axis).bit_length() - 1)]


def neighbours(lower, upper, axis):
    size = lax.axis_size(axis)
    even = lax.axis_index(axis) % 2 == 0
    within, across = [], []
    for i in range(0, size, 2):
        within += [(i, i + 1), (i + 1, i)]
        across += [(i + 1, (i + 2) % size), ((i + 2) % size, i + 1)]
    far = lax.ppermute(jnp.where(even, lower, upper), axis, across)
    close = lax.ppermute(jnp.where(even, upper, lower), axis, within)
    return jnp.where(even, far, close), jnp.where(even, close, far)


def together(*xs):
    return lax.optimization_barrier(xs)


def per_device(
    collocation, source, wall_index, bc_type, bc_value,
    in_weight, local_weight, local_bias, trunk_weight, trunk_bias, head_weight,
):
    rows, cols = lax.axis_size("sx"), lax.axis_size("sy")
    assert rows & (rows - 1) == 0 and cols & (cols - 1) == 0 and rows >= 4 and cols >= 2
    points, edge, width = collocation.shape[2], wall_index.shape[2], local_weight.shape[1]
    rims_total = 4 * edge
    inner_count = float(points * rows * cols)
    wall_count = float(rims_total * rows * cols)

    core = ("sy", 0)
    halved = (("sx", 0), ("sx", 1), core)
    doubled = [b for b in bits_of("sy") + bits_of("sx") if b not in halved]
    order_size = 1 << len(halved)

    def mine():
        return sum(((lax.axis_index(axis) >> bit) & 1) << k for k, (axis, bit) in enumerate(halved))

    big = shape(width, width)
    small = shape(8, width)

    def stack(count, size, dtype=F32):
        return shape(count, size, width, dtype=dtype)

    def vm(s):
        return pltpu.VMEM(s.shape, s.dtype)

    entry_weight = jnp.transpose(in_weight, (1, 0, 2))
    firsts = (wall_index, entry_weight, local_weight, local_bias, trunk_weight, trunk_bias, head_weight)
    (rims, sw, tw, a0w, x0w, z1w, x1w, z2w) = call(
        wall_forward_kernel,
        (
            shape(4, 2 * edge), shape(rims_total, LANES), shape(rims_total, LANES),
            shape(rims_total, width), stack(2, rims_total, BF16), stack(2, rims_total),
            stack(2, rims_total, BF16), stack(2, rims_total),
        ),
        [pltpu.VMEM((rims_total, LANES), F32)] * 2
        + [pltpu.SemaphoreType.DMA((len(firsts),))]
        + [vm(x) for x in firsts],
        tuple(pltpu.with_memory_space_constraint(x, pltpu.HBM) for x in firsts),
        4 * rims_total * 2 * width * width,
        pltpu.HBM,
    )
    south, north = neighbours(rims[2:3], rims[3:4], "sy")
    west, east = neighbours(rims[0:1], rims[1:2], "sx")

    (grad_r, isums, si, ti, a0i, x0i, z1i, g2i) = call(
        functools.partial(inner_kernel, order_size, mine),
        (
            big, small, shape(points, LANES), shape(points, LANES), shape(points, width),
            stack(5, points, BF16), stack(5, points), stack(5, points, BF16),
        ),
        [vm(stack(5, points, BF16)), vm(stack(5, points)), pltpu.VMEM((points, LANES), F32)],
        (collocation, source, entry_weight, local_weight, local_bias, trunk_weight, trunk_bias, head_weight),
        6 * points * 5 * width * width,
    )
    (grad_b, sums, wheads, g2w) = call(
        functools.partial(wall_top_kernel, order_size, mine, rows),
        (big, small, shape(1, width), stack(2, rims_total, BF16)),
        [pltpu.VMEM((rims_total, LANES), F32)] * 2,
        (rims, west, east, south, north, bc_type.T, bc_value, z2w, x1w, head_weight, isums),
        2 * rims_total * 2 * width * width,
    )
    half = width // 2
    got_r = swap(grad_r[half:], *core)
    grad_r = grad_r[:half] + got_r
    more = swap(sums, *core)
    sums = sums + more
    got_b = swap(grad_b[half:], *core)
    grad_b = grad_b[:half] + got_b
    part = half // 4
    gots = []
    for mask in (1, 2, 3):
        where = slice(mask * part, (mask + 1) * part)
        trio = []
        for x in (sums, grad_r[where], grad_b[where]):
            trio.append(exchange(x, "sx", mask))
        gots.append(trio)
    sums = sums + gots[0][0] + gots[1][0] + gots[2][0]
    keep_r = grad_r[:part] + gots[0][1] + gots[1][1] + gots[2][1]
    keep_b = grad_b[:part] + gots[0][2] + gots[1][2] + gots[2][2]
    sums, g2w = together(sums, g2w)
    for axis, bit in doubled:
        more = swap(sums, axis, bit)
        sums = sums + more
    gi, gw, biases = call(
        hidden_kernel,
        (stack(5, points, BF16), stack(2, rims_total, BF16), small),
        [vm(stack(4, points)), vm(stack(2, rims_total))],
        (trunk_weight, z1i, g2i, z1w, g2w),
        2 * (points * 4 + rims_total * 2) * width * width,
    )
    fr, fb, _ = factors(sums[2:3], sums[3:4], inner_count, wall_count)
    block = fr * keep_r + fb * keep_b
    block, biases = together(block, biases)
    for axis, bit in doubled[:1]:
        block = block + swap(block, axis, bit)
    parts = call(
        entry_kernel,
        small,
        [vm(stack(4, points)), vm(stack(2, rims_total))],
        (entry_weight, local_weight, si, ti, a0i, gi, sw, tw, a0w, gw, biases),
        2 * (points * 4 + rims_total * 2) * width * width,
    )
    block, parts = together(block, parts)
    for axis, bit in doubled[1:]:
        block = block + swap(block, axis, bit)
    in_grad, local_grad, local_bias_grad, head_grad, trunk_bias_grad, loss = call(
        functools.partial(blend_kernel, inner_count, wall_count),
        (shape(3, 1, width), shape(1, width, width)) + (shape(1, width),) * 3 + (shape(1, 1),),
        [],
        (sums, parts, isums, wheads, x0i, gi, x0w, gw),
        2 * (points * 5 + rims_total * 2) * width * width,
    )
    blocks = [block]
    for mask in (1, 2, 3):
        blocks.append(exchange(block, "sx", mask))
    *blocks, local_bias_grad = together(*blocks, local_bias_grad)
    blocks = blocks + [swap(b, *core) for b in blocks]
    trunk_grad = call(
        functools.partial(unorder_kernel, order_size, mine),
        shape(1, width, width),
        [],
        tuple(blocks),
        width * width,
    )
    return (
        trunk_grad, trunk_bias_grad, jnp.transpose(in_grad, (1, 0, 2)), local_grad,
        local_bias_grad, head_grad, loss.reshape(()),
    )


def solution(mesh):
    return jax.shard_map(
        per_device,
        mesh=mesh,
        in_specs=(
            P(None, "sx", "sy"),
            P("sx", "sy"),
            P(None, "sx", "sy"),
            P(None, "sy"),
            P(None, "sy"),
            P("sx", None, "sy"),
            P("sx", None, "sy"),
            P("sx", "sy"),
            P(),
            P(),
            P("sx", "sy"),
        ),
        out_specs=(
            P(),
            P(),
            P("sx", None, "sy"),
            P("sx", None, "sy"),
            P("sx", "sy"),
            P("sx", "sy"),
            P(),
        ),
        check_vma=False,
    )
```

profile of v0, /device:TPU:0, one launch (start us, length us, event | category | flops | bytes accessed | tf_op | source)
XLA Modules:
  0.0 71.1 jit_solution(3903624729460514472)
XLA Ops:
  0.7 2.9 %shard_map.162 = (f32[4,128]{1,0:T(4,128)S(1)}, f32[256,128]{1,0:T(8,128)S(1)}, f32[256,128]{1,0:T(8,128)S(1)}, f32[256,512]{1,0:T(8,128)S(1)}, bf16[2,256,512]{...) custom-call(s32[4,1,64]{2,1,0:T(1,128)} %refs_0_.1, ...), custom_call_target="tpu_custom_call" | custom-call | flops 536870912 | tf_op jit(solution)/shard_map/pallas_call | solution.py:496
  3.7 3.0 %collective-permute-start.1 = (f32[1,128]{1,0:T(1,128)S(1)}, f32[1,128]{1,0:T(1,128)S(1)}, u32[]{:S(2)}, u32[]{:S(2)}) collective-permute-start(f32[1,128]{1,0:T(1,128)S(1)} %get-tuple-element.95), channel_id=1, source_target_pairs={{0,8},{8,0},{16,24},{24,16},{1,9},{9,1},{17,25},{25,17},{2,10},{10... | collective-permute-start | bytes 1544 | tf_op jit(solution)/shard_map/ppermute | solution.py:531
  6.7 1.5 %collective-permute-start = (f32[1,128]{1,0:T(1,128)S(1)}, f32[1,128]{1,0:T(1,128)S(1)}, u32[]{:S(2)}, u32[]{:S(2)}) collective-permute-start(f32[1,128]{1,0:T(1,128)S(1)} %get-tuple-element.94), channel_id=1, source_target_pairs={{8,16},{16,8},{24,0},{0,24},{9,17},{17,9},{25,1},{1,25},{10,18},{1... | collective-permute-start | bytes 1544 | tf_op jit(solution)/shard_map/ppermute | solution.py:530
  8.2 3.7 %collective-permute-start.2 = (f32[1,128]{1,0:T(1,128)S(1)}, f32[1,128]{1,0:T(1,128)S(1)}, u32[]{:S(2)}, u32[]{:S(2)}) collective-permute-start(f32[1,128]{1,0:T(1,128)S(1)} %get-tuple-element.96), channel_id=1, source_target_pairs={{1,2},{2,1},{3,4},{4,3},{5,6},{6,5},{7,0},{0,7},{9,10},{10,9},{11,... | collective-permute-start | bytes 1544 | tf_op jit(solution)/shard_map/ppermute | solution.py:530
  12.0 4.8 %shard_map.163 = (f32[512,512]{1,0:T(8,128)S(1)}, f32[8,512]{1,0:T(8,128)S(1)}, f32[256,128]{1,0:T(8,128)S(1)}, f32[256,128]{1,0:T(8,128)S(1)}, f32[256,512]{1,0...) custom-call(f32[2,1,256]{2,1,0:T(1,128)S(1)} %copy-done.8, ...), custom_call_target="tpu_custom_call" | custom-call | flops 2013265920 | tf_op jit(solution)/shard_map/pallas_call | solution.py:496
  17.0 1.4 %shard_map.164 = (f32[512,512]{1,0:T(8,128)S(1)}, f32[8,512]{1,0:T(8,128)S(1)}, f32[1,512]{1,0:T(1,128)S(1)}, bf16[2,256,512]{2,1,0:T(8,128)(2,1)S(1)}) custom-call(f32[4,128]{1,0:T(4,128)S(1)} %get-tuple-element.47.rims_ref, f32[1,128]{1,0:T(1,128)S(1)} %get-tuple-element.100.west_ref, f32[1,128]{1,0:T(1,128)S(1)} %get-tuple-element.99.east_ref, ...), custom_call_target="tpu_custom_call" | custom-call | flops 268435456 | tf_op jit(solution)/shard_map/pallas_call | solution.py:496
  19.8 1.4 %collective-permute-start.7 = (f32[8,512]{1,0:T(8,128)S(1)}, f32[8,512]{1,0:T(8,128)S(1)}, u32[]{:S(2)}, u32[]{:S(2)}) collective-permute-start(f32[8,512]{1,0:T(8,128)S(1)} %add.66), channel_id=1, source_target_pairs={{0,24},{8,16},{16,8},{24,0},{1,25},{9,17},{17,9},{25,1},{2,26},{10... | collective-permute-start | bytes 49160 | tf_op jit(solution)/shard_map/ppermute | solution.py:516
  21.3 1.5 %collective-permute-start.6 = (f32[8,512]{1,0:T(8,128)S(1)}, f32[8,512]{1,0:T(8,128)S(1)}, u32[]{:S(2)}, u32[]{:S(2)}) collective-permute-start(f32[8,512]{1,0:T(8,128)S(1)} %add.66), channel_id=1, source_target_pairs={{0,16},{8,24},{16,0},{24,8},{1,17},{9,25},{17,1},{25,9},{2,18},{10... | collective-permute-start | bytes 49160 | tf_op jit(solution)/shard_map/ppermute | solution.py:516
  25.0 1.5 %collective-permute-done.5 = f32[8,512]{1,0:T(8,128)S(1)} collective-permute-done((f32[8,512]{1,0:T(8,128)S(1)}, f32[8,512]{1,0:T(8,128)S(1)}, u32[]{:S(2)}, u32[]{:S(2)}) %collective-permute-start.5) | collective-permute-done | bytes 16416 | tf_op jit(solution)/shard_map/ppermute | solution.py:516
  26.7 3.6 %collective-permute-done.8 = f32[8,512]{1,0:T(8,128)S(1)} collective-permute-done((f32[8,512]{1,0:T(8,128)S(1)}, f32[8,512]{1,0:T(8,128)S(1)}, u32[]{:S(2)}, u32[]{:S(2)}) %collective-permute-start.8) | collective-permute-done | bytes 16416 | tf_op jit(solution)/shard_map/ppermute | solution.py:516
  30.7 2.3 %shard_map.165 = (bf16[5,256,512]{2,1,0:T(8,128)(2,1)S(1)}, bf16[2,256,512]{2,1,0:T(8,128)(2,1)S(1)}, f32[8,512]{1,0:T(8,128)S(1)}) custom-call(bf16[1,512,512]{2,1,0:T(8,128)(2,1)S(1)} %copy-done, f32[5,256,512]{2,1,0:T(8,128)S(1)} %get-tuple-element.56.z1i_ref, bf16[5,256,512]{2,1,0:T(8,128)(2,1)S(1)} %get-tuple-element.57.g2i_ref, ...), custom_call_target="tpu_custom_call" | custom-call | flops 805306368 | tf_op jit(solution)/shard_map/pallas_call | solution.py:496
  33.0 1.9 %collective-permute-done.9 = f32[8,512]{1,0:T(8,128)S(1)} collective-permute-done((f32[8,512]{1,0:T(8,128)S(1)}, f32[8,512]{1,0:T(8,128)S(1)}, u32[]{:S(2)}, u32[]{:S(2)}) %collective-permute-start.9) | collective-permute-done | bytes 16416 | tf_op jit(solution)/shard_map/ppermute | solution.py:516
  35.6 1.5 %collective-permute-start.12 = (f32[64,512]{1,0:T(8,128)S(1)}, f32[64,512]{1,0:T(8,128)S(1)}, u32[]{:S(2)}, u32[]{:S(2)}) collective-permute-start(f32[64,512]{1,0:T(8,128)S(1)} %get-tuple-element.89), channel_id=1, source_target_pairs={{0,16},{8,24},{16,0},{24,8},{1,17},{9,25},{17,1},{25,9},{2,18},{10... | collective-permute-start | bytes 393224 | tf_op jit(solution)/shard_map/ppermute | solution.py:516
  37.1 1.5 %collective-permute-start.11 = (f32[64,512]{1,0:T(8,128)S(1)}, f32[64,512]{1,0:T(8,128)S(1)}, u32[]{:S(2)}, u32[]{:S(2)}) collective-permute-start(f32[64,512]{1,0:T(8,128)S(1)} %get-tuple-element.87), channel_id=1, source_target_pairs={{0,8},{8,0},{16,24},{24,16},{1,9},{9,1},{17,25},{25,17},{2,10},{10... | collective-permute-start | bytes 393224 | tf_op jit(solution)/shard_map/ppermute | solution.py:516
  39.3 1.5 %collective-permute-start.16 = (f32[64,512]{1,0:T(8,128)S(1)}, f32[64,512]{1,0:T(8,128)S(1)}, u32[]{:S(2)}, u32[]{:S(2)}) collective-permute-start(f32[64,512]{1,0:T(8,128)S(1)} %get-tuple-element.92), channel_id=1, source_target_pairs={{0,16},{8,24},{16,0},{24,8},{1,17},{9,25},{17,1},{25,9},{2,18},{10... | collective-permute-start | bytes 393224 | tf_op jit(solution)/shard_map/ppermute | solution.py:516
  40.8 1.3 %collective-permute-done.13 = f32[64,512]{1,0:T(8,128)S(1)} collective-permute-done((f32[64,512]{1,0:T(8,128)S(1)}, f32[64,512]{1,0:T(8,128)S(1)}, u32[]{:S(2)}, u32[]{:S(2)}) %collective-permute-start.13) | collective-permute-done | bytes 131104 | tf_op jit(solution)/shard_map/ppermute | solution.py:516
  43.0 1.9 %collective-permute-done.17 = f32[64,512]{1,0:T(8,128)S(1)} collective-permute-done((f32[64,512]{1,0:T(8,128)S(1)}, f32[64,512]{1,0:T(8,128)S(1)}, u32[]{:S(2)}, u32[]{:S(2)}) %collective-permute-start.17) | collective-permute-done | bytes 131104 | tf_op jit(solution)/shard_map/ppermute | solution.py:516
  47.6 2.5 %shard_map.166.parts_ref = f32[8,512]{1,0:T(8,128)S(1)} custom-call(f32[3,1,512]{2,1,0:T(1,128)S(1)} %bitcast.7, bf16[1,512,512]{2,1,0:T(8,128)(2,1)S(1)} %copy-done.1, f32[256,128]{1,0:T(8,128)S(1)} %get-tuple-element.62.si_ref, f32[256,128]{1,0:T(8,128)S(1)} %get-tuple-element.63.ti_ref, f32[256,512]{1,0:T(8,128)S(1)} %get-tuple-element.64.a0i_ref, ...), custom_call_target="tpu_custom_call" | custom-call | flops 805306368 | tf_op jit(solution)/shard_map/pallas_call | solution.py:496
  50.0 3.3 %collective-permute-done.18 = f32[64,512]{1,0:T(8,128)S(1)} collective-permute-done((f32[64,512]{1,0:T(8,128)S(1)}, f32[64,512]{1,0:T(8,128)S(1)}, u32[]{:S(2)}, u32[]{:S(2)}) %collective-permute-start.18) | collective-permute-done | bytes 131104 | tf_op jit(solution)/shard_map/ppermute | solution.py:516
  54.3 6.1 %collective-permute-done.19 = f32[64,512]{1,0:T(8,128)S(1)} collective-permute-done((f32[64,512]{1,0:T(8,128)S(1)}, f32[64,512]{1,0:T(8,128)S(1)}, u32[]{:S(2)}, u32[]{:S(2)}) %collective-permute-start.19) | collective-permute-done | bytes 131104 | tf_op jit(solution)/shard_map/ppermute | solution.py:516
  60.8 1.3 %collective-permute-start.21 = (f32[64,512]{1,0:T(8,128)S(1)}, f32[64,512]{1,0:T(8,128)S(1)}, u32[]{:S(2)}, u32[]{:S(2)}) collective-permute-start(f32[64,512]{1,0:T(8,128)S(1)} %add.84.refs_0_), channel_id=1, source_target_pairs={{0,16},{8,24},{16,0},{24,8},{1,17},{9,25},{17,1},{25,9},{2,18},{10... | collective-permute-start | bytes 393224 | tf_op jit(solution)/shard_map/ppermute | solution.py:516
  62.1 1.9 %collective-permute-start.22 = (f32[64,512]{1,0:T(8,128)S(1)}, f32[64,512]{1,0:T(8,128)S(1)}, u32[]{:S(2)}, u32[]{:S(2)}) collective-permute-start(f32[64,512]{1,0:T(8,128)S(1)} %add.84.refs_0_), channel_id=1, source_target_pairs={{0,24},{8,16},{16,8},{24,0},{1,25},{9,17},{17,9},{25,1},{2,26},{10... | collective-permute-start | bytes 393224 | tf_op jit(solution)/shard_map/ppermute | solution.py:516
  64.0 2.1 %shard_map.167 = (f32[3,1,512]{2,1,0:T(1,128)}, f32[1,512,512]{2,1,0:T(8,128)}, f32[1,512]{1,0:T(1,128)}, f32[1,512]{1,0:T(1,128)}, f32[1,512]{1,0:T(1,128)}, /*index=5*/f32[1,1]{1,0:T(1,128)}) custom-call(f32[8,512]{1,0:T(8,128)S(1)} %add.71.sums_ref, f32[8,512]{1,0:T(8,128)S(1)} %shard_map.166.parts_ref, f32[8,512]{1,0:T(8,128)S(1)} %get-tuple-element.50.isums_ref, ...), custom_call_target="tpu_custom_call" | custom-call | flops 939524096 | tf_op jit(solution)/shard_map/pallas_call | solution.py:496
  66.2 1.8 %collective-permute-done.22.refs_3_ = f32[64,512]{1,0:T(8,128)S(1)} collective-permute-done((f32[64,512]{1,0:T(8,128)S(1)}, f32[64,512]{1,0:T(8,128)S(1)}, u32[]{:S(2)}, u32[]{:S(2)}) %collective-permute-start.22) | collective-permute-done | bytes 131104 | tf_op jit(solution)/shard_map/ppermute | solution.py:516
  (74 shorter events, 13.6 us)
Async XLA Ops:
  3.7 13.3 %collective-permute-start.1 = (f32[1,128]{1,0:T(1,128)S(1)}, f32[1,128]{1,0:T(1,128)S(1)}, u32[]{:S(2)}, u32[]{:S(2)}) collective-permute-start(f32[1,128]{1,0:T(1,128)S(1)} %get-tuple-element.95), channel_id=1, source_target_pairs={{0,8},{8,0},{16,24},{24,16},{1,9},{9,1},{17,25},{25,17},{2,10},{10... | collective-permute-start | bytes 1544 | tf_op jit(solution)/shard_map/ppermute | solution.py:531
  6.7 10.2 %collective-permute-start = (f32[1,128]{1,0:T(1,128)S(1)}, f32[1,128]{1,0:T(1,128)S(1)}, u32[]{:S(2)}, u32[]{:S(2)}) collective-permute-start(f32[1,128]{1,0:T(1,128)S(1)} %get-tuple-element.94), channel_id=1, source_target_pairs={{8,16},{16,8},{24,0},{0,24},{9,17},{17,9},{25,1},{1,25},{10,18},{1... | collective-permute-start | bytes 1544 | tf_op jit(solution)/shard_map/ppermute | solution.py:530
  8.2 8.8 %collective-permute-start.3 = (f32[1,128]{1,0:T(1,128)S(1)}, f32[1,128]{1,0:T(1,128)S(1)}, u32[]{:S(2)}, u32[]{:S(2)}) collective-permute-start(f32[1,128]{1,0:T(1,128)S(1)} %get-tuple-element.93), channel_id=1, source_target_pairs={{0,1},{1,0},{2,3},{3,2},{4,5},{5,4},{6,7},{7,6},{8,9},{9,8},{10,11... | collective-permute-start | bytes 1544 | tf_op jit(solution)/shard_map/ppermute | solution.py:531
  8.2 8.8 %collective-permute-start.2 = (f32[1,128]{1,0:T(1,128)S(1)}, f32[1,128]{1,0:T(1,128)S(1)}, u32[]{:S(2)}, u32[]{:S(2)}) collective-permute-start(f32[1,128]{1,0:T(1,128)S(1)} %get-tuple-element.96), channel_id=1, source_target_pairs={{1,2},{2,1},{3,4},{4,3},{5,6},{6,5},{7,0},{0,7},{9,10},{10,9},{11,... | collective-permute-start | bytes 1544 | tf_op jit(solution)/shard_map/ppermute | solution.py:530
  16.9 18.1 %collective-permute-start.10 = (f32[256,512]{1,0:T(8,128)S(1)}, f32[256,512]{1,0:T(8,128)S(1)}, u32[]{:S(2)}, u32[]{:S(2)}) collective-permute-start(f32[256,512]{1,0:T(8,128)S(1)} %slice.61), channel_id=1, source_target_pairs={{0,1},{1,0},{2,3},{3,2},{4,5},{5,4},{6,7},{7,6},{8,9},{9,8},{10,11... | collective-permute-start | bytes 1572872 | tf_op jit(solution)/shard_map/ppermute | solution.py:516
  19.8 4.6 %collective-permute-start.7 = (f32[8,512]{1,0:T(8,128)S(1)}, f32[8,512]{1,0:T(8,128)S(1)}, u32[]{:S(2)}, u32[]{:S(2)}) collective-permute-start(f32[8,512]{1,0:T(8,128)S(1)} %add.66), channel_id=1, source_target_pairs={{0,24},{8,16},{16,8},{24,0},{1,25},{9,17},{17,9},{25,1},{2,26},{10... | collective-permute-start | bytes 49160 | tf_op jit(solution)/shard_map/ppermute | solution.py:516
  21.3 3.7 %collective-permute-start.6 = (f32[8,512]{1,0:T(8,128)S(1)}, f32[8,512]{1,0:T(8,128)S(1)}, u32[]{:S(2)}, u32[]{:S(2)}) collective-permute-start(f32[8,512]{1,0:T(8,128)S(1)} %add.66), channel_id=1, source_target_pairs={{0,16},{8,24},{16,0},{24,8},{1,17},{9,25},{17,1},{25,9},{2,18},{10... | collective-permute-start | bytes 49160 | tf_op jit(solution)/shard_map/ppermute | solution.py:516
  22.8 3.7 %collective-permute-start.5 = (f32[8,512]{1,0:T(8,128)S(1)}, f32[8,512]{1,0:T(8,128)S(1)}, u32[]{:S(2)}, u32[]{:S(2)}) collective-permute-start(f32[8,512]{1,0:T(8,128)S(1)} %add.66), channel_id=1, source_target_pairs={{0,8},{8,0},{16,24},{24,16},{1,9},{9,1},{17,25},{25,17},{2,10},{10... | collective-permute-start | bytes 49160 | tf_op jit(solution)/shard_map/ppermute | solution.py:516
  26.5 3.7 %collective-permute-start.8 = (f32[8,512]{1,0:T(8,128)S(1)}, f32[8,512]{1,0:T(8,128)S(1)}, u32[]{:S(2)}, u32[]{:S(2)}) collective-permute-start(f32[8,512]{1,0:T(8,128)S(1)} %add_add_fusion), channel_id=1, source_target_pairs={{0,2},{1,3},{2,0},{3,1},{4,6},{5,7},{6,4},{7,5},{8,10},{9,11},{10,... | collective-permute-start | bytes 49160 | tf_op jit(solution)/shard_map/ppermute | solution.py:516
  26.6 12.0 %collective-permute-start.14 = (f32[256,512]{1,0:T(8,128)S(1)}, f32[256,512]{1,0:T(8,128)S(1)}, u32[]{:S(2)}, u32[]{:S(2)}) collective-permute-start(f32[256,512]{1,0:T(8,128)S(1)} %slice.67), channel_id=1, source_target_pairs={{0,1},{1,0},{2,3},{3,2},{4,5},{5,4},{6,7},{7,6},{8,9},{9,8},{10,11... | collective-permute-start | bytes 1572872 | tf_op jit(solution)/shard_map/ppermute | solution.py:516
  30.3 4.6 %collective-permute-start.9 = (f32[8,512]{1,0:T(8,128)S(1)}, f32[8,512]{1,0:T(8,128)S(1)}, u32[]{:S(2)}, u32[]{:S(2)}) collective-permute-start(f32[8,512]{1,0:T(8,128)S(1)} %add.70), channel_id=1, source_target_pairs={{0,4},{1,5},{2,6},{3,7},{4,0},{5,1},{6,2},{7,3},{8,12},{9,13},{10,... | collective-permute-start | bytes 49160 | tf_op jit(solution)/shard_map/ppermute | solution.py:516
  35.0 7.0 %collective-permute-start.13 = (f32[64,512]{1,0:T(8,128)S(1)}, f32[64,512]{1,0:T(8,128)S(1)}, u32[]{:S(2)}, u32[]{:S(2)}) collective-permute-start(f32[64,512]{1,0:T(8,128)S(1)} %get-tuple-element.88), channel_id=1, source_target_pairs={{0,24},{8,16},{16,8},{24,0},{1,25},{9,17},{17,9},{25,1},{2,26},{10... | collective-permute-start | bytes 393224 | tf_op jit(solution)/shard_map/ppermute | solution.py:516
  35.6 7.4 %collective-permute-start.12 = (f32[64,512]{1,0:T(8,128)S(1)}, f32[64,512]{1,0:T(8,128)S(1)}, u32[]{:S(2)}, u32[]{:S(2)}) collective-permute-start(f32[64,512]{1,0:T(8,128)S(1)} %get-tuple-element.89), channel_id=1, source_target_pairs={{0,16},{8,24},{16,0},{24,8},{1,17},{9,25},{17,1},{25,9},{2,18},{10... | collective-permute-start | bytes 393224 | tf_op jit(solution)/shard_map/ppermute | solution.py:516
  37.1 5.9 %collective-permute-start.11 = (f32[64,512]{1,0:T(8,128)S(1)}, f32[64,512]{1,0:T(8,128)S(1)}, u32[]{:S(2)}, u32[]{:S(2)}) collective-permute-start(f32[64,512]{1,0:T(8,128)S(1)} %get-tuple-element.87), channel_id=1, source_target_pairs={{0,8},{8,0},{16,24},{24,16},{1,9},{9,1},{17,25},{25,17},{2,10},{10... | collective-permute-start | bytes 393224 | tf_op jit(solution)/shard_map/ppermute | solution.py:516
  38.7 6.2 %collective-permute-start.17 = (f32[64,512]{1,0:T(8,128)S(1)}, f32[64,512]{1,0:T(8,128)S(1)}, u32[]{:S(2)}, u32[]{:S(2)}) collective-permute-start(f32[64,512]{1,0:T(8,128)S(1)} %get-tuple-element.91), channel_id=1, source_target_pairs={{0,24},{8,16},{16,8},{24,0},{1,25},{9,17},{17,9},{25,1},{2,26},{10... | collective-permute-start | bytes 393224 | tf_op jit(solution)/shard_map/ppermute | solution.py:516
  39.3 6.6 %collective-permute-start.16 = (f32[64,512]{1,0:T(8,128)S(1)}, f32[64,512]{1,0:T(8,128)S(1)}, u32[]{:S(2)}, u32[]{:S(2)}) collective-permute-start(f32[64,512]{1,0:T(8,128)S(1)} %get-tuple-element.92), channel_id=1, source_target_pairs={{0,16},{8,24},{16,0},{24,8},{1,17},{9,25},{17,1},{25,9},{2,18},{10... | collective-permute-start | bytes 393224 | tf_op jit(solution)/shard_map/ppermute | solution.py:516
  42.1 5.0 %collective-permute-start.15 = (f32[64,512]{1,0:T(8,128)S(1)}, f32[64,512]{1,0:T(8,128)S(1)}, u32[]{:S(2)}, u32[]{:S(2)}) collective-permute-start(f32[64,512]{1,0:T(8,128)S(1)} %get-tuple-element.90), channel_id=1, source_target_pairs={{0,8},{8,0},{16,24},{24,16},{1,9},{9,1},{17,25},{25,17},{2,10},{10... | collective-permute-start | bytes 393224 | tf_op jit(solution)/shard_map/ppermute | solution.py:516
  47.1 6.2 %collective-permute-start.18 = (f32[64,512]{1,0:T(8,128)S(1)}, f32[64,512]{1,0:T(8,128)S(1)}, u32[]{:S(2)}, u32[]{:S(2)}) collective-permute-start(f32[64,512]{1,0:T(8,128)S(1)} %fusion.3), channel_id=1, source_target_pairs={{0,2},{1,3},{2,0},{3,1},{4,6},{5,7},{6,4},{7,5},{8,10},{9,11},{10,... | collective-permute-start | bytes 393224 | tf_op jit(solution)/shard_map/ppermute | solution.py:516
  53.3 7.1 %collective-permute-start.19 = (f32[64,512]{1,0:T(8,128)S(1)}, f32[64,512]{1,0:T(8,128)S(1)}, u32[]{:S(2)}, u32[]{:S(2)}) collective-permute-start(f32[64,512]{1,0:T(8,128)S(1)} %add.83), channel_id=1, source_target_pairs={{0,4},{1,5},{2,6},{3,7},{4,0},{5,1},{6,2},{7,3},{8,12},{9,13},{10,... | collective-permute-start | bytes 393224 | tf_op jit(solution)/shard_map/ppermute | solution.py:516
  60.5 5.7 %collective-permute-start.20 = (f32[64,512]{1,0:T(8,128)S(1)}, f32[64,512]{1,0:T(8,128)S(1)}, u32[]{:S(2)}, u32[]{:S(2)}) collective-permute-start(f32[64,512]{1,0:T(8,128)S(1)} %add.84.refs_0_), channel_id=1, source_target_pairs={{0,8},{8,0},{16,24},{24,16},{1,9},{9,1},{17,25},{25,17},{2,10},{10... | collective-permute-start | bytes 393224 | tf_op jit(solution)/shard_map/ppermute | solution.py:516
  60.8 5.4 %collective-permute-start.21 = (f32[64,512]{1,0:T(8,128)S(1)}, f32[64,512]{1,0:T(8,128)S(1)}, u32[]{:S(2)}, u32[]{:S(2)}) collective-permute-start(f32[64,512]{1,0:T(8,128)S(1)} %add.84.refs_0_), channel_id=1, source_target_pairs={{0,16},{8,24},{16,0},{24,8},{1,17},{9,25},{17,1},{25,9},{2,18},{10... | collective-permute-start | bytes 393224 | tf_op jit(solution)/shard_map/ppermute | solution.py:516
  62.1 5.9 %collective-permute-start.22 = (f32[64,512]{1,0:T(8,128)S(1)}, f32[64,512]{1,0:T(8,128)S(1)}, u32[]{:S(2)}, u32[]{:S(2)}) collective-permute-start(f32[64,512]{1,0:T(8,128)S(1)} %add.84.refs_0_), channel_id=1, source_target_pairs={{0,24},{8,16},{16,8},{24,0},{1,25},{9,17},{17,9},{25,1},{2,26},{10... | collective-permute-start | bytes 393224 | tf_op jit(solution)/shard_map/ppermute | solution.py:516
  68.0 1.5 %collective-permute-start.24 = (f32[64,512]{1,0:T(8,128)S(1)}, f32[64,512]{1,0:T(8,128)S(1)}, u32[]{:S(2)}, u32[]{:S(2)}) collective-permute-start(f32[64,512]{1,0:T(8,128)S(1)} %collective-permute-done.20.refs_1_), channel_id=1, source_target_pairs={{0,1},{1,0},{2,3},{3,2},{4,5},{5,4},{6,7},{7,6},{8,9},{9,8},{10,11... | collective-permute-start | bytes 393224 | tf_op jit(solution)/shard_map/ppermute | solution.py:516
  68.5 1.5 %collective-permute-start.26 = (f32[64,512]{1,0:T(8,128)S(1)}, f32[64,512]{1,0:T(8,128)S(1)}, u32[]{:S(2)}, u32[]{:S(2)}) collective-permute-start(f32[64,512]{1,0:T(8,128)S(1)} %collective-permute-done.22.refs_3_), channel_id=1, source_target_pairs={{0,1},{1,0},{2,3},{3,2},{4,5},{5,4},{6,7},{7,6},{8,9},{9,8},{10,11... | collective-permute-start | bytes 393224 | tf_op jit(solution)/shard_map/ppermute | solution.py:516
  (13 other events, 111.8 us)
where the time goes:
time: 71.2 us; the launch traced here: 71.1 us
  waiting for transfers between devices  27.2 us (38%)
  starting transfers between devices  25.3 us (36%)
  Pallas kernels  17.1 us (24%)
  between operations  0.96 us (1%)
    ppermute x23, waiting for transfers between devices, exchange(): lax.ppermute(x, axis, [(i, i ^ mask) for i in range(lax.axis_size(axis))])  27.2 us
    pallas_call x7, Pallas kernels, call(): pl.pallas_call(kernel, out_shape=outs, in_specs=[pl.BlockSpec(memory_spac...  17.1 us
    ppermute x23, starting transfers between devices, exchange(): lax.ppermute(x, axis, [(i, i ^ mask) for i in range(lax.axis_size(axis))])  17.1 us
    ppermute x2, starting transfers between devices, neighbours(): far = lax.ppermute(jnp.where(even, lower, upper), axis, across)  5.2 us
    ppermute x2, starting transfers between devices, neighbours(): close = lax.ppermute(jnp.where(even, upper, lower), axis, within)  3.04 us
  transfers between devices with their start and end apart: 27, of which 18 were waited for; matrix products, arithmetic and copies ran while one was open for 0% of the time, Pallas kernels for 18%

commit v1 on v0

--- a/solution.py
+++ b/solution.py
@@ -611,13 +611,14 @@
     gots = []
     for mask in (1, 2, 3):
         where = slice(mask * part, (mask + 1) * part)
-        trio = []
-        for x in (sums, grad_r[where], grad_b[where]):
-            trio.append(exchange(x, "sx", mask))
-        gots.append(trio)
+        pair = []
+        for x in (sums, jnp.concatenate([grad_r[where], grad_b[where]], axis=0)):
+            pair.append(exchange(x, "sx", mask))
+        gots.append(pair)
     sums = sums + gots[0][0] + gots[1][0] + gots[2][0]
-    keep_r = grad_r[:part] + gots[0][1] + gots[1][1] + gots[2][1]
-    keep_b = grad_b[:part] + gots[0][2] + gots[1][2] + gots[2][2]
+    both = gots[0][1] + gots[1][1] + gots[2][1]
+    keep_r = grad_r[:part] + both[:part]
+    keep_b = grad_b[:part] + both[part:]
     sums, g2w = together(sums, g2w)
     for axis, bit in doubled:
         more = swap(sums, axis, bit)

time: 71.2 us -> 66.2 us (0.930)
  waiting for transfers between devices: 27.2 us -> 22 us
    ppermute x23 -> x20, waiting for transfers between devices: 27.2 us -> 22 us  [exchange(): lax.ppermute(x, axis, [(i, i ^ mask) for i in range(lax.axis_size(axis))])]
    ppermute x23 -> x20, starting transfers between devices: 17.1 us -> 17.1 us  [exchange(): lax.ppermute(x, axis, [(i, i ^ mask) for i in range(lax.axis_size(axis))])]
  transfers between devices with their start and end apart: 27 -> 24, of which waited for: 18 -> 16; matrix products, arithmetic and copies ran while one was open for 0% -> 1% of each run, Pallas kernels for 18% -> 20%
where the time goes in v1:
time: 66.2 us; the launch traced here: 66 us
  starting transfers between devices  25.4 us (38%)
  waiting for transfers between devices  22 us (33%)
  Pallas kernels  17.1 us (26%)
  between operations  0.99 us (1%)
    ppermute x20, waiting for transfers between devices, exchange(): lax.ppermute(x, axis, [(i, i ^ mask) for i in range(lax.axis_size(axis))])  22 us
    ppermute x20, starting transfers between devices, exchange(): lax.ppermute(x, axis, [(i, i ^ mask) for i in range(lax.axis_size(axis))])  17.1 us
    pallas_call x7, Pallas kernels, call(): pl.pallas_call(kernel, out_shape=outs, in_specs=[pl.BlockSpec(memory_spac...  17.1 us
    ppermute x2, starting transfers between devices, neighbours(): far = lax.ppermute(jnp.where(even, lower, upper), axis, across)  5.2 us
    ppermute x2, starting transfers between devices, neighbours(): close = lax.ppermute(jnp.where(even, upper, lower), axis, within)  3.04 us
  transfers between devices with their start and end apart: 24, of which 16 were waited for; matrix products, arithmetic and copies ran while one was open for 1% of the time, Pallas kernels for 20%

profile of v1, /device:TPU:0, one launch (start us, length us, event | category | flops | bytes accessed | tf_op | source)
XLA Modules:
  0.0 66.0 jit_solution(9834553453789181330)
XLA Ops:
  0.7 2.9 %shard_map.162 = (f32[4,128]{1,0:T(4,128)S(1)}, f32[256,128]{1,0:T(8,128)S(1)}, f32[256,128]{1,0:T(8,128)S(1)}, f32[256,512]{1,0:T(8,128)S(1)}, bf16[2,256,512]{...) custom-call(s32[4,1,64]{2,1,0:T(1,128)} %refs_0_.1, ...), custom_call_target="tpu_custom_call" | custom-call | flops 536870912 | tf_op jit(solution)/shard_map/pallas_call | solution.py:496
  3.7 3.0 %collective-permute-start.1 = (f32[1,128]{1,0:T(1,128)S(1)}, f32[1,128]{1,0:T(1,128)S(1)}, u32[]{:S(2)}, u32[]{:S(2)}) collective-permute-start(f32[1,128]{1,0:T(1,128)S(1)} %get-tuple-element.95), channel_id=1, source_target_pairs={{0,8},{8,0},{16,24},{24,16},{1,9},{9,1},{17,25},{25,17},{2,10},{10... | collective-permute-start | bytes 1544 | tf_op jit(solution)/shard_map/ppermute | solution.py:531
  6.7 1.5 %collective-permute-start = (f32[1,128]{1,0:T(1,128)S(1)}, f32[1,128]{1,0:T(1,128)S(1)}, u32[]{:S(2)}, u32[]{:S(2)}) collective-permute-start(f32[1,128]{1,0:T(1,128)S(1)} %get-tuple-element.94), channel_id=1, source_target_pairs={{8,16},{16,8},{24,0},{0,24},{9,17},{17,9},{25,1},{1,25},{10,18},{1... | collective-permute-start | bytes 1544 | tf_op jit(solution)/shard_map/ppermute | solution.py:530
  8.2 3.7 %collective-permute-start.2 = (f32[1,128]{1,0:T(1,128)S(1)}, f32[1,128]{1,0:T(1,128)S(1)}, u32[]{:S(2)}, u32[]{:S(2)}) collective-permute-start(f32[1,128]{1,0:T(1,128)S(1)} %get-tuple-element.96), channel_id=1, source_target_pairs={{1,2},{2,1},{3,4},{4,3},{5,6},{6,5},{7,0},{0,7},{9,10},{10,9},{11,... | collective-permute-start | bytes 1544 | tf_op jit(solution)/shard_map/ppermute | solution.py:530
  12.0 4.8 %shard_map.163 = (f32[512,512]{1,0:T(8,128)S(1)}, f32[8,512]{1,0:T(8,128)S(1)}, f32[256,128]{1,0:T(8,128)S(1)}, f32[256,128]{1,0:T(8,128)S(1)}, f32[256,512]{1,0...) custom-call(f32[2,1,256]{2,1,0:T(1,128)S(1)} %copy-done.8, ...), custom_call_target="tpu_custom_call" | custom-call | flops 2013265920 | tf_op jit(solution)/shard_map/pallas_call | solution.py:496
  17.0 1.4 %shard_map.164 = (f32[512,512]{1,0:T(8,128)S(1)}, f32[8,512]{1,0:T(8,128)S(1)}, f32[1,512]{1,0:T(1,128)S(1)}, bf16[2,256,512]{2,1,0:T(8,128)(2,1)S(1)}) custom-call(f32[4,128]{1,0:T(4,128)S(1)} %get-tuple-element.47.rims_ref, f32[1,128]{1,0:T(1,128)S(1)} %get-tuple-element.100.west_ref, f32[1,128]{1,0:T(1,128)S(1)} %get-tuple-element.99.east_ref, ...), custom_call_target="tpu_custom_call" | custom-call | flops 268435456 | tf_op jit(solution)/shard_map/pallas_call | solution.py:496
  19.8 1.4 %collective-permute-start.7 = (f32[8,512]{1,0:T(8,128)S(1)}, f32[8,512]{1,0:T(8,128)S(1)}, u32[]{:S(2)}, u32[]{:S(2)}) collective-permute-start(f32[8,512]{1,0:T(8,128)S(1)} %add.60), channel_id=1, source_target_pairs={{0,24},{8,16},{16,8},{24,0},{1,25},{9,17},{17,9},{25,1},{2,26},{10... | collective-permute-start | bytes 49160 | tf_op jit(solution)/shard_map/ppermute | solution.py:516
  21.3 1.5 %collective-permute-start.6 = (f32[8,512]{1,0:T(8,128)S(1)}, f32[8,512]{1,0:T(8,128)S(1)}, u32[]{:S(2)}, u32[]{:S(2)}) collective-permute-start(f32[8,512]{1,0:T(8,128)S(1)} %add.60), channel_id=1, source_target_pairs={{0,16},{8,24},{16,0},{24,8},{1,17},{9,25},{17,1},{25,9},{2,18},{10... | collective-permute-start | bytes 49160 | tf_op jit(solution)/shard_map/ppermute | solution.py:516
  23.4 1.0 %collective-permute-done.7 = f32[8,512]{1,0:T(8,128)S(1)} collective-permute-done((f32[8,512]{1,0:T(8,128)S(1)}, f32[8,512]{1,0:T(8,128)S(1)}, u32[]{:S(2)}, u32[]{:S(2)}) %collective-permute-start.7) | collective-permute-done | bytes 16416 | tf_op jit(solution)/shard_map/ppermute | solution.py:516
  25.0 1.5 %collective-permute-done.5 = f32[8,512]{1,0:T(8,128)S(1)} collective-permute-done((f32[8,512]{1,0:T(8,128)S(1)}, f32[8,512]{1,0:T(8,128)S(1)}, u32[]{:S(2)}, u32[]{:S(2)}) %collective-permute-start.5) | collective-permute-done | bytes 16416 | tf_op jit(solution)/shard_map/ppermute | solution.py:516
  26.5 3.7 %collective-permute-done.8 = f32[8,512]{1,0:T(8,128)S(1)} collective-permute-done((f32[8,512]{1,0:T(8,128)S(1)}, f32[8,512]{1,0:T(8,128)S(1)}, u32[]{:S(2)}, u32[]{:S(2)}) %collective-permute-start.8) | collective-permute-done | bytes 16416 | tf_op jit(solution)/shard_map/ppermute | solution.py:516
  31.5 1.6 %collective-permute-start.12 = (f32[128,512]{1,0:T(8,128)S(1)}, f32[128,512]{1,0:T(8,128)S(1)}, u32[]{:S(2)}, u32[]{:S(2)}) collective-permute-start(f32[128,512]{1,0:T(8,128)S(1)} %pad_maximum_fusion), channel_id=1, source_target_pairs={{0,8},{8,0},{16,24},{24,16},{1,9},{9,1},{17,25},{25,17},{2,10},{10... | collective-permute-start | bytes 786440 | tf_op jit(solution)/shard_map/ppermute | solution.py:516
  33.1 1.6 %collective-permute-start.13 = (f32[128,512]{1,0:T(8,128)S(1)}, f32[128,512]{1,0:T(8,128)S(1)}, u32[]{:S(2)}, u32[]{:S(2)}) collective-permute-start(f32[128,512]{1,0:T(8,128)S(1)} %pad_maximum_fusion.1), channel_id=1, source_target_pairs={{0,16},{8,24},{16,0},{24,8},{1,17},{9,25},{17,1},{25,9},{2,18},{10... | collective-permute-start | bytes 786440 | tf_op jit(solution)/shard_map/ppermute | solution.py:516
  34.7 2.3 %shard_map.165 = (bf16[5,256,512]{2,1,0:T(8,128)(2,1)S(1)}, bf16[2,256,512]{2,1,0:T(8,128)(2,1)S(1)}, f32[8,512]{1,0:T(8,128)S(1)}) custom-call(bf16[1,512,512]{2,1,0:T(8,128)(2,1)S(1)} %copy-done, f32[5,256,512]{2,1,0:T(8,128)S(1)} %get-tuple-element.56.z1i_ref, bf16[5,256,512]{2,1,0:T(8,128)(2,1)S(1)} %get-tuple-element.57.g2i_ref, ...), custom_call_target="tpu_custom_call" | custom-call | flops 805306368 | tf_op jit(solution)/shard_map/pallas_call | solution.py:496
  37.0 3.2 %collective-permute-done.14 = f32[128,512]{1,0:T(8,128)S(1)} collective-permute-done((f32[128,512]{1,0:T(8,128)S(1)}, f32[128,512]{1,0:T(8,128)S(1)}, u32[]{:S(2)}, u32[]{:S(2)}) %collective-permute-start.14) | collective-permute-done | bytes 262176 | tf_op jit(solution)/shard_map/ppermute | solution.py:516
  40.2 1.7 %collective-permute-done.12 = f32[128,512]{1,0:T(8,128)S(1)} collective-permute-done((f32[128,512]{1,0:T(8,128)S(1)}, f32[128,512]{1,0:T(8,128)S(1)}, u32[]{:S(2)}, u32[]{:S(2)}) %collective-permute-start.12) | collective-permute-done | bytes 262176 | tf_op jit(solution)/shard_map/ppermute | solution.py:516
  43.8 2.5 %shard_map.166.parts_ref = f32[8,512]{1,0:T(8,128)S(1)} custom-call(f32[3,1,512]{2,1,0:T(1,128)S(1)} %bitcast.7, bf16[1,512,512]{2,1,0:T(8,128)(2,1)S(1)} %copy-done.1, f32[256,128]{1,0:T(8,128)S(1)} %get-tuple-element.62.si_ref, f32[256,128]{1,0:T(8,128)S(1)} %get-tuple-element.63.ti_ref, f32[256,512]{1,0:T(8,128)S(1)} %get-tuple-element.64.a0i_ref, ...), custom_call_target="tpu_custom_call" | custom-call | flops 805306368 | tf_op jit(solution)/shard_map/pallas_call | solution.py:496
  46.2 1.9 %collective-permute-done.15 = f32[64,512]{1,0:T(8,128)S(1)} collective-permute-done((f32[64,512]{1,0:T(8,128)S(1)}, f32[64,512]{1,0:T(8,128)S(1)}, u32[]{:S(2)}, u32[]{:S(2)}) %collective-permute-start.15) | collective-permute-done | bytes 131104 | tf_op jit(solution)/shard_map/ppermute | solution.py:516
  48.1 3.6 %collective-permute-start.16 = (f32[64,512]{1,0:T(8,128)S(1)}, f32[64,512]{1,0:T(8,128)S(1)}, u32[]{:S(2)}, u32[]{:S(2)}) collective-permute-start(f32[64,512]{1,0:T(8,128)S(1)} %add.75), channel_id=1, source_target_pairs={{0,4},{1,5},{2,6},{3,7},{4,0},{5,1},{6,2},{7,3},{8,12},{9,13},{10,... | collective-permute-start | bytes 393224 | tf_op jit(solution)/shard_map/ppermute | solution.py:516
  51.7 3.8 %collective-permute-done.16 = f32[64,512]{1,0:T(8,128)S(1)} collective-permute-done((f32[64,512]{1,0:T(8,128)S(1)}, f32[64,512]{1,0:T(8,128)S(1)}, u32[]{:S(2)}, u32[]{:S(2)}) %collective-permute-start.16) | collective-permute-done | bytes 131104 | tf_op jit(solution)/shard_map/ppermute | solution.py:516
  57.0 2.0 %collective-permute-start.19 = (f32[64,512]{1,0:T(8,128)S(1)}, f32[64,512]{1,0:T(8,128)S(1)}, u32[]{:S(2)}, u32[]{:S(2)}) collective-permute-start(f32[64,512]{1,0:T(8,128)S(1)} %add.76.refs_0_), channel_id=1, source_target_pairs={{0,24},{8,16},{16,8},{24,0},{1,25},{9,17},{17,9},{25,1},{2,26},{10... | collective-permute-start | bytes 393224 | tf_op jit(solution)/shard_map/ppermute | solution.py:516
  59.1 2.1 %shard_map.167 = (f32[3,1,512]{2,1,0:T(1,128)}, f32[1,512,512]{2,1,0:T(8,128)}, f32[1,512]{1,0:T(1,128)}, f32[1,512]{1,0:T(1,128)}, f32[1,512]{1,0:T(1,128)}, /*index=5*/f32[1,1]{1,0:T(1,128)}) custom-call(f32[8,512]{1,0:T(8,128)S(1)} %add.65.sums_ref, f32[8,512]{1,0:T(8,128)S(1)} %shard_map.166.parts_ref, f32[8,512]{1,0:T(8,128)S(1)} %get-tuple-element.50.isums_ref, ...), custom_call_target="tpu_custom_call" | custom-call | flops 939524096 | tf_op jit(solution)/shard_map/pallas_call | solution.py:496
  61.4 1.5 %collective-permute-done.19.refs_3_ = f32[64,512]{1,0:T(8,128)S(1)} collective-permute-done((f32[64,512]{1,0:T(8,128)S(1)}, f32[64,512]{1,0:T(8,128)S(1)}, u32[]{:S(2)}, u32[]{:S(2)}) %collective-permute-start.19) | collective-permute-done | bytes 131104 | tf_op jit(solution)/shard_map/ppermute | solution.py:516
  65.0 1.1 %shard_map.168 = f32[1,512,512]{2,1,0:T(8,128)} custom-call(f32[64,512]{1,0:T(8,128)S(1)} %add.76.refs_0_, f32[64,512]{1,0:T(8,128)S(1)} %collective-permute-done.17.refs_1_, f32[64,512]{1,0:T(8,128)S(1)} %collective-permute-done.18.refs_2_, f32[64,512]{1,0:T(8,128)S(1)} %collective-permute-done.19.refs_3_, f32[64,512]{1,0:T(8,128)S(1)} %collective-permute-done.20.refs_4_, ...), custom_call_target="tpu_custom_call" | custom-call | flops 262144 | tf_op jit(solution)/shard_map/pallas_call | solution.py:496
  (72 shorter events, 9.6 us)
Async XLA Ops:
  3.7 13.3 %collective-permute-start.1 = (f32[1,128]{1,0:T(1,128)S(1)}, f32[1,128]{1,0:T(1,128)S(1)}, u32[]{:S(2)}, u32[]{:S(2)}) collective-permute-start(f32[1,128]{1,0:T(1,128)S(1)} %get-tuple-element.95), channel_id=1, source_target_pairs={{0,8},{8,0},{16,24},{24,16},{1,9},{9,1},{17,25},{25,17},{2,10},{10... | collective-permute-start | bytes 1544 | tf_op jit(solution)/shard_map/ppermute | solution.py:531
  6.7 10.2 %collective-permute-start = (f32[1,128]{1,0:T(1,128)S(1)}, f32[1,128]{1,0:T(1,128)S(1)}, u32[]{:S(2)}, u32[]{:S(2)}) collective-permute-start(f32[1,128]{1,0:T(1,128)S(1)} %get-tuple-element.94), channel_id=1, source_target_pairs={{8,16},{16,8},{24,0},{0,24},{9,17},{17,9},{25,1},{1,25},{10,18},{1... | collective-permute-start | bytes 1544 | tf_op jit(solution)/shard_map/ppermute | solution.py:530
  8.2 8.8 %collective-permute-start.3 = (f32[1,128]{1,0:T(1,128)S(1)}, f32[1,128]{1,0:T(1,128)S(1)}, u32[]{:S(2)}, u32[]{:S(2)}) collective-permute-start(f32[1,128]{1,0:T(1,128)S(1)} %get-tuple-element.93), channel_id=1, source_target_pairs={{0,1},{1,0},{2,3},{3,2},{4,5},{5,4},{6,7},{7,6},{8,9},{9,8},{10,11... | collective-permute-start | bytes 1544 | tf_op jit(solution)/shard_map/ppermute | solution.py:531
  8.2 8.8 %collective-permute-start.2 = (f32[1,128]{1,0:T(1,128)S(1)}, f32[1,128]{1,0:T(1,128)S(1)}, u32[]{:S(2)}, u32[]{:S(2)}) collective-permute-start(f32[1,128]{1,0:T(1,128)S(1)} %get-tuple-element.96), channel_id=1, source_target_pairs={{1,2},{2,1},{3,4},{4,3},{5,6},{6,5},{7,0},{0,7},{9,10},{10,9},{11,... | collective-permute-start | bytes 1544 | tf_op jit(solution)/shard_map/ppermute | solution.py:530
  16.9 13.8 %collective-permute-start.10 = (f32[256,512]{1,0:T(8,128)S(1)}, f32[256,512]{1,0:T(8,128)S(1)}, u32[]{:S(2)}, u32[]{:S(2)}) collective-permute-start(f32[256,512]{1,0:T(8,128)S(1)} %slice.67), channel_id=1, source_target_pairs={{0,1},{1,0},{2,3},{3,2},{4,5},{5,4},{6,7},{7,6},{8,9},{9,8},{10,11... | collective-permute-start | bytes 1572872 | tf_op jit(solution)/shard_map/ppermute | solution.py:516
  18.4 1.4 %collective-permute-start.4 = (f32[8,512]{1,0:T(8,128)S(1)}, f32[8,512]{1,0:T(8,128)S(1)}, u32[]{:S(2)}, u32[]{:S(2)}) collective-permute-start(f32[8,512]{1,0:T(8,128)S(1)} %get-tuple-element.51), channel_id=1, source_target_pairs={{0,1},{1,0},{2,3},{3,2},{4,5},{5,4},{6,7},{7,6},{8,9},{9,8},{10,11... | collective-permute-start | bytes 49160 | tf_op jit(solution)/shard_map/ppermute | solution.py:516
  19.8 4.6 %collective-permute-start.7 = (f32[8,512]{1,0:T(8,128)S(1)}, f32[8,512]{1,0:T(8,128)S(1)}, u32[]{:S(2)}, u32[]{:S(2)}) collective-permute-start(f32[8,512]{1,0:T(8,128)S(1)} %add.60), channel_id=1, source_target_pairs={{0,24},{8,16},{16,8},{24,0},{1,25},{9,17},{17,9},{25,1},{2,26},{10... | collective-permute-start | bytes 49160 | tf_op jit(solution)/shard_map/ppermute | solution.py:516
  21.3 3.7 %collective-permute-start.6 = (f32[8,512]{1,0:T(8,128)S(1)}, f32[8,512]{1,0:T(8,128)S(1)}, u32[]{:S(2)}, u32[]{:S(2)}) collective-permute-start(f32[8,512]{1,0:T(8,128)S(1)} %add.60), channel_id=1, source_target_pairs={{0,16},{8,24},{16,0},{24,8},{1,17},{9,25},{17,1},{25,9},{2,18},{10... | collective-permute-start | bytes 49160 | tf_op jit(solution)/shard_map/ppermute | solution.py:516
  22.8 3.7 %collective-permute-start.5 = (f32[8,512]{1,0:T(8,128)S(1)}, f32[8,512]{1,0:T(8,128)S(1)}, u32[]{:S(2)}, u32[]{:S(2)}) collective-permute-start(f32[8,512]{1,0:T(8,128)S(1)} %add.60), channel_id=1, source_target_pairs={{0,8},{8,0},{16,24},{24,16},{1,9},{9,1},{17,25},{25,17},{2,10},{10... | collective-permute-start | bytes 49160 | tf_op jit(solution)/shard_map/ppermute | solution.py:516
  23.4 7.4 %collective-permute-start.11 = (f32[256,512]{1,0:T(8,128)S(1)}, f32[256,512]{1,0:T(8,128)S(1)}, u32[]{:S(2)}, u32[]{:S(2)}) collective-permute-start(f32[256,512]{1,0:T(8,128)S(1)} %slice.71), channel_id=1, source_target_pairs={{0,1},{1,0},{2,3},{3,2},{4,5},{5,4},{6,7},{7,6},{8,9},{9,8},{10,11... | collective-permute-start | bytes 1572872 | tf_op jit(solution)/shard_map/ppermute | solution.py:516
  26.5 3.7 %collective-permute-start.8 = (f32[8,512]{1,0:T(8,128)S(1)}, f32[8,512]{1,0:T(8,128)S(1)}, u32[]{:S(2)}, u32[]{:S(2)}) collective-permute-start(f32[8,512]{1,0:T(8,128)S(1)} %add_add_fusion.1), channel_id=1, source_target_pairs={{0,2},{1,3},{2,0},{3,1},{4,6},{5,7},{6,4},{7,5},{8,10},{9,11},{10,... | collective-permute-start | bytes 49160 | tf_op jit(solution)/shard_map/ppermute | solution.py:516
  30.3 6.7 %collective-permute-start.9 = (f32[8,512]{1,0:T(8,128)S(1)}, f32[8,512]{1,0:T(8,128)S(1)}, u32[]{:S(2)}, u32[]{:S(2)}) collective-permute-start(f32[8,512]{1,0:T(8,128)S(1)} %add.64), channel_id=1, source_target_pairs={{0,4},{1,5},{2,6},{3,7},{4,0},{5,1},{6,2},{7,3},{8,12},{9,13},{10,... | collective-permute-start | bytes 49160 | tf_op jit(solution)/shard_map/ppermute | solution.py:516
  31.0 9.3 %collective-permute-start.14 = (f32[128,512]{1,0:T(8,128)S(1)}, f32[128,512]{1,0:T(8,128)S(1)}, u32[]{:S(2)}, u32[]{:S(2)}) collective-permute-start(f32[128,512]{1,0:T(8,128)S(1)} %pad_maximum_fusion.2), channel_id=1, source_target_pairs={{0,24},{8,16},{16,8},{24,0},{1,25},{9,17},{17,9},{25,1},{2,26},{10... | collective-permute-start | bytes 786440 | tf_op jit(solution)/shard_map/ppermute | solution.py:516
  31.5 10.4 %collective-permute-start.12 = (f32[128,512]{1,0:T(8,128)S(1)}, f32[128,512]{1,0:T(8,128)S(1)}, u32[]{:S(2)}, u32[]{:S(2)}) collective-permute-start(f32[128,512]{1,0:T(8,128)S(1)} %pad_maximum_fusion), channel_id=1, source_target_pairs={{0,8},{8,0},{16,24},{24,16},{1,9},{9,1},{17,25},{25,17},{2,10},{10... | collective-permute-start | bytes 786440 | tf_op jit(solution)/shard_map/ppermute | solution.py:516
  33.1 9.8 %collective-permute-start.13 = (f32[128,512]{1,0:T(8,128)S(1)}, f32[128,512]{1,0:T(8,128)S(1)}, u32[]{:S(2)}, u32[]{:S(2)}) collective-permute-start(f32[128,512]{1,0:T(8,128)S(1)} %pad_maximum_fusion.1), channel_id=1, source_target_pairs={{0,16},{8,24},{16,0},{24,8},{1,17},{9,25},{17,1},{25,9},{2,18},{10... | collective-permute-start | bytes 786440 | tf_op jit(solution)/shard_map/ppermute | solution.py:516
  43.0 5.0 %collective-permute-start.15 = (f32[64,512]{1,0:T(8,128)S(1)}, f32[64,512]{1,0:T(8,128)S(1)}, u32[]{:S(2)}, u32[]{:S(2)}) collective-permute-start(f32[64,512]{1,0:T(8,128)S(1)} %fusion.1), channel_id=1, source_target_pairs={{0,2},{1,3},{2,0},{3,1},{4,6},{5,7},{6,4},{7,5},{8,10},{9,11},{10,... | collective-permute-start | bytes 393224 | tf_op jit(solution)/shard_map/ppermute | solution.py:516
  48.1 7.4 %collective-permute-start.16 = (f32[64,512]{1,0:T(8,128)S(1)}, f32[64,512]{1,0:T(8,128)S(1)}, u32[]{:S(2)}, u32[]{:S(2)}) collective-permute-start(f32[64,512]{1,0:T(8,128)S(1)} %add.75), channel_id=1, source_target_pairs={{0,4},{1,5},{2,6},{3,7},{4,0},{5,1},{6,2},{7,3},{8,12},{9,13},{10,... | collective-permute-start | bytes 393224 | tf_op jit(solution)/shard_map/ppermute | solution.py:516
  55.5 5.7 %collective-permute-start.17 = (f32[64,512]{1,0:T(8,128)S(1)}, f32[64,512]{1,0:T(8,128)S(1)}, u32[]{:S(2)}, u32[]{:S(2)}) collective-permute-start(f32[64,512]{1,0:T(8,128)S(1)} %add.76.refs_0_), channel_id=1, source_target_pairs={{0,8},{8,0},{16,24},{24,16},{1,9},{9,1},{17,25},{25,17},{2,10},{10... | collective-permute-start | bytes 393224 | tf_op jit(solution)/shard_map/ppermute | solution.py:516
  56.4 5.0 %collective-permute-start.18 = (f32[64,512]{1,0:T(8,128)S(1)}, f32[64,512]{1,0:T(8,128)S(1)}, u32[]{:S(2)}, u32[]{:S(2)}) collective-permute-start(f32[64,512]{1,0:T(8,128)S(1)} %add.76.refs_0_), channel_id=1, source_target_pairs={{0,16},{8,24},{16,0},{24,8},{1,17},{9,25},{17,1},{25,9},{2,18},{10... | collective-permute-start | bytes 393224 | tf_op jit(solution)/shard_map/ppermute | solution.py:516
  57.0 5.9 %collective-permute-start.19 = (f32[64,512]{1,0:T(8,128)S(1)}, f32[64,512]{1,0:T(8,128)S(1)}, u32[]{:S(2)}, u32[]{:S(2)}) collective-permute-start(f32[64,512]{1,0:T(8,128)S(1)} %add.76.refs_0_), channel_id=1, source_target_pairs={{0,24},{8,16},{16,8},{24,0},{1,25},{9,17},{17,9},{25,1},{2,26},{10... | collective-permute-start | bytes 393224 | tf_op jit(solution)/shard_map/ppermute | solution.py:516
  62.9 1.3 %collective-permute-start.20 = (f32[64,512]{1,0:T(8,128)S(1)}, f32[64,512]{1,0:T(8,128)S(1)}, u32[]{:S(2)}, u32[]{:S(2)}) collective-permute-start(f32[64,512]{1,0:T(8,128)S(1)} %add.76.refs_0_), channel_id=1, source_target_pairs={{0,1},{1,0},{2,3},{3,2},{4,5},{5,4},{6,7},{7,6},{8,9},{9,8},{10,11... | collective-permute-start | bytes 393224 | tf_op jit(solution)/shard_map/ppermute | solution.py:516
  62.9 1.5 %collective-permute-start.21 = (f32[64,512]{1,0:T(8,128)S(1)}, f32[64,512]{1,0:T(8,128)S(1)}, u32[]{:S(2)}, u32[]{:S(2)}) collective-permute-start(f32[64,512]{1,0:T(8,128)S(1)} %collective-permute-done.17.refs_1_), channel_id=1, source_target_pairs={{0,1},{1,0},{2,3},{3,2},{4,5},{5,4},{6,7},{7,6},{8,9},{9,8},{10,11... | collective-permute-start | bytes 393224 | tf_op jit(solution)/shard_map/ppermute | solution.py:516
  63.4 1.3 %collective-permute-start.22 = (f32[64,512]{1,0:T(8,128)S(1)}, f32[64,512]{1,0:T(8,128)S(1)}, u32[]{:S(2)}, u32[]{:S(2)}) collective-permute-start(f32[64,512]{1,0:T(8,128)S(1)} %collective-permute-done.18.refs_2_), channel_id=1, source_target_pairs={{0,1},{1,0},{2,3},{3,2},{4,5},{5,4},{6,7},{7,6},{8,9},{9,8},{10,11... | collective-permute-start | bytes 393224 | tf_op jit(solution)/shard_map/ppermute | solution.py:516
  63.4 1.5 %collective-permute-start.23 = (f32[64,512]{1,0:T(8,128)S(1)}, f32[64,512]{1,0:T(8,128)S(1)}, u32[]{:S(2)}, u32[]{:S(2)}) collective-permute-start(f32[64,512]{1,0:T(8,128)S(1)} %collective-permute-done.19.refs_3_), channel_id=1, source_target_pairs={{0,1},{1,0},{2,3},{3,2},{4,5},{5,4},{6,7},{7,6},{8,9},{9,8},{10,11... | collective-permute-start | bytes 393224 | tf_op jit(solution)/shard_map/ppermute | solution.py:516
  (10 other events, 107.7 us)

commit v2 on v1

--- a/solution.py
+++ b/solution.py
@@ -340,12 +340,17 @@
 
 
 def unorder_kernel(order_size, order_of, *refs):
-    ins, out_ref = refs[:order_size], refs[order_size]
+    ins, out_ref, sems = refs[:order_size], refs[order_size], refs[order_size + 1]
     size = ins[0].shape[0]
     mine = order_of()
+    copies = []
     for place, ref in enumerate(ins):
         where = pl.ds(pl.multiple_of((mine ^ place) * size, size), size)
-        out_ref[0, where, :] = ref[...]
+        copies.append(pltpu.make_async_copy(ref, out_ref.at[0, where, :], sems.at[place]))
+    for copy in copies:
+        copy.start()
+    for copy in copies:
+        copy.wait()
 
 
 def back(g_ref, count, weight, u_ref):
@@ -491,8 +496,8 @@
     ) + fb * tn(x0w_ref[...].reshape(2 * rims, width), gw_ref[...].reshape(2 * rims, width))
 
 
-def call(kernel, outs, scratch, args, flops, space=pltpu.VMEM):
-    vmem = pl.BlockSpec(memory_space=pltpu.VMEM)
+def call(kernel, outs, scratch, args, flops, space=pltpu.VMEM, into=pltpu.VMEM):
+    vmem = pl.BlockSpec(memory_space=into)
     return pl.pallas_call(
         kernel,
         out_shape=outs,
@@ -660,9 +665,10 @@
     trunk_grad = call(
         functools.partial(unorder_kernel, order_size, mine),
         shape(1, width, width),
-        [],
+        [pltpu.SemaphoreType.DMA((order_size,))],
         tuple(blocks),
         width * width,
+        into=pltpu.HBM,
     )
     return (
         trunk_grad, trunk_bias_grad, jnp.transpose(in_grad, (1, 0, 2)), local_grad,

time: 66.2 us -> 66.1 us (level)
  no operation moved by 1% of the time
where the time goes in v2:
time: 66.1 us; the launch traced here: 66 us
  starting transfers between devices  25.4 us (38%)
  waiting for transfers between devices  22 us (33%)
  Pallas kernels  17.1 us (26%)
  between operations  0.99 us (1%)
    ppermute x20, waiting for transfers between devices, exchange(): lax.ppermute(x, axis, [(i, i ^ mask) for i in range(lax.axis_size(axis))])  22 us
    ppermute x20, starting transfers between devices, exchange(): lax.ppermute(x, axis, [(i, i ^ mask) for i in range(lax.axis_size(axis))])  17.1 us
    pallas_call x7, Pallas kernels, call(): pl.pallas_call(kernel, out_shape=outs, in_specs=[pl.BlockSpec(memory_spac...  17.1 us
    ppermute x2, starting transfers between devices, neighbours(): far = lax.ppermute(jnp.where(even, lower, upper), axis, across)  5.2 us
    ppermute x2, starting transfers between devices, neighbours(): close = lax.ppermute(jnp.where(even, upper, lower), axis, within)  3.04 us
  transfers between devices with their start and end apart: 24, of which 16 were waited for; matrix products, arithmetic and copies ran while one was open for 1% of the time, Pallas kernels for 20%

profile of v2, /device:TPU:0, one launch (start us, length us, event | category | flops | bytes accessed | tf_op | source)
XLA Modules:
  0.0 66.0 jit_solution(11273962815799445960)
XLA Ops:
  0.7 2.9 %shard_map.162 = (f32[4,128]{1,0:T(4,128)S(1)}, f32[256,128]{1,0:T(8,128)S(1)}, f32[256,128]{1,0:T(8,128)S(1)}, f32[256,512]{1,0:T(8,128)S(1)}, bf16[2,256,512]{...) custom-call(s32[4,1,64]{2,1,0:T(1,128)} %refs_0_.1, ...), custom_call_target="tpu_custom_call" | custom-call | flops 536870912 | tf_op jit(solution)/shard_map/pallas_call | solution.py:501
  3.7 3.0 %collective-permute-start.1 = (f32[1,128]{1,0:T(1,128)S(1)}, f32[1,128]{1,0:T(1,128)S(1)}, u32[]{:S(2)}, u32[]{:S(2)}) collective-permute-start(f32[1,128]{1,0:T(1,128)S(1)} %get-tuple-element.95), channel_id=1, source_target_pairs={{0,8},{8,0},{16,24},{24,16},{1,9},{9,1},{17,25},{25,17},{2,10},{10... | collective-permute-start | bytes 1544 | tf_op jit(solution)/shard_map/ppermute | solution.py:536
  6.7 1.5 %collective-permute-start = (f32[1,128]{1,0:T(1,128)S(1)}, f32[1,128]{1,0:T(1,128)S(1)}, u32[]{:S(2)}, u32[]{:S(2)}) collective-permute-start(f32[1,128]{1,0:T(1,128)S(1)} %get-tuple-element.94), channel_id=1, source_target_pairs={{8,16},{16,8},{24,0},{0,24},{9,17},{17,9},{25,1},{1,25},{10,18},{1... | collective-permute-start | bytes 1544 | tf_op jit(solution)/shard_map/ppermute | solution.py:535
  8.2 3.7 %collective-permute-start.2 = (f32[1,128]{1,0:T(1,128)S(1)}, f32[1,128]{1,0:T(1,128)S(1)}, u32[]{:S(2)}, u32[]{:S(2)}) collective-permute-start(f32[1,128]{1,0:T(1,128)S(1)} %get-tuple-element.96), channel_id=1, source_target_pairs={{1,2},{2,1},{3,4},{4,3},{5,6},{6,5},{7,0},{0,7},{9,10},{10,9},{11,... | collective-permute-start | bytes 1544 | tf_op jit(solution)/shard_map/ppermute | solution.py:535
  12.0 4.8 %shard_map.163 = (f32[512,512]{1,0:T(8,128)S(1)}, f32[8,512]{1,0:T(8,128)S(1)}, f32[256,128]{1,0:T(8,128)S(1)}, f32[256,128]{1,0:T(8,128)S(1)}, f32[256,512]{1,0...) custom-call(f32[2,1,256]{2,1,0:T(1,128)S(1)} %copy-done.8, ...), custom_call_target="tpu_custom_call" | custom-call | flops 2013265920 | tf_op jit(solution)/shard_map/pallas_call | solution.py:501
  17.0 1.4 %shard_map.164 = (f32[512,512]{1,0:T(8,128)S(1)}, f32[8,512]{1,0:T(8,128)S(1)}, f32[1,512]{1,0:T(1,128)S(1)}, bf16[2,256,512]{2,1,0:T(8,128)(2,1)S(1)}) custom-call(f32[4,128]{1,0:T(4,128)S(1)} %get-tuple-element.47.rims_ref, f32[1,128]{1,0:T(1,128)S(1)} %get-tuple-element.100.west_ref, f32[1,128]{1,0:T(1,128)S(1)} %get-tuple-element.99.east_ref, ...), custom_call_target="tpu_custom_call" | custom-call | flops 268435456 | tf_op jit(solution)/shard_map/pallas_call | solution.py:501
  19.8 1.4 %collective-permute-start.7 = (f32[8,512]{1,0:T(8,128)S(1)}, f32[8,512]{1,0:T(8,128)S(1)}, u32[]{:S(2)}, u32[]{:S(2)}) collective-permute-start(f32[8,512]{1,0:T(8,128)S(1)} %add.60), channel_id=1, source_target_pairs={{0,24},{8,16},{16,8},{24,0},{1,25},{9,17},{17,9},{25,1},{2,26},{10... | collective-permute-start | bytes 49160 | tf_op jit(solution)/shard_map/ppermute | solution.py:521
  21.3 1.5 %collective-permute-start.6 = (f32[8,512]{1,0:T(8,128)S(1)}, f32[8,512]{1,0:T(8,128)S(1)}, u32[]{:S(2)}, u32[]{:S(2)}) collective-permute-start(f32[8,512]{1,0:T(8,128)S(1)} %add.60), channel_id=1, source_target_pairs={{0,16},{8,24},{16,0},{24,8},{1,17},{9,25},{17,1},{25,9},{2,18},{10... | collective-permute-start | bytes 49160 | tf_op jit(solution)/shard_map/ppermute | solution.py:521
  23.4 1.0 %collective-permute-done.7 = f32[8,512]{1,0:T(8,128)S(1)} collective-permute-done((f32[8,512]{1,0:T(8,128)S(1)}, f32[8,512]{1,0:T(8,128)S(1)}, u32[]{:S(2)}, u32[]{:S(2)}) %collective-permute-start.7) | collective-permute-done | bytes 16416 | tf_op jit(solution)/shard_map/ppermute | solution.py:521
  25.0 1.5 %collective-permute-done.5 = f32[8,512]{1,0:T(8,128)S(1)} collective-permute-done((f32[8,512]{1,0:T(8,128)S(1)}, f32[8,512]{1,0:T(8,128)S(1)}, u32[]{:S(2)}, u32[]{:S(2)}) %collective-permute-start.5) | collective-permute-done | bytes 16416 | tf_op jit(solution)/shard_map/ppermute | solution.py:521
  26.5 3.7 %collective-permute-done.8 = f32[8,512]{1,0:T(8,128)S(1)} collective-permute-done((f32[8,512]{1,0:T(8,128)S(1)}, f32[8,512]{1,0:T(8,128)S(1)}, u32[]{:S(2)}, u32[]{:S(2)}) %collective-permute-start.8) | collective-permute-done | bytes 16416 | tf_op jit(solution)/shard_map/ppermute | solution.py:521
  31.5 1.6 %collective-permute-start.12 = (f32[128,512]{1,0:T(8,128)S(1)}, f32[128,512]{1,0:T(8,128)S(1)}, u32[]{:S(2)}, u32[]{:S(2)}) collective-permute-start(f32[128,512]{1,0:T(8,128)S(1)} %pad_maximum_fusion), channel_id=1, source_target_pairs={{0,8},{8,0},{16,24},{24,16},{1,9},{9,1},{17,25},{25,17},{2,10},{10... | collective-permute-start | bytes 786440 | tf_op jit(solution)/shard_map/ppermute | solution.py:521
  33.1 1.6 %collective-permute-start.13 = (f32[128,512]{1,0:T(8,128)S(1)}, f32[128,512]{1,0:T(8,128)S(1)}, u32[]{:S(2)}, u32[]{:S(2)}) collective-permute-start(f32[128,512]{1,0:T(8,128)S(1)} %pad_maximum_fusion.1), channel_id=1, source_target_pairs={{0,16},{8,24},{16,0},{24,8},{1,17},{9,25},{17,1},{25,9},{2,18},{10... | collective-permute-start | bytes 786440 | tf_op jit(solution)/shard_map/ppermute | solution.py:521
  34.7 2.3 %shard_map.165 = (bf16[5,256,512]{2,1,0:T(8,128)(2,1)S(1)}, bf16[2,256,512]{2,1,0:T(8,128)(2,1)S(1)}, f32[8,512]{1,0:T(8,128)S(1)}) custom-call(bf16[1,512,512]{2,1,0:T(8,128)(2,1)S(1)} %copy-done, f32[5,256,512]{2,1,0:T(8,128)S(1)} %get-tuple-element.56.z1i_ref, bf16[5,256,512]{2,1,0:T(8,128)(2,1)S(1)} %get-tuple-element.57.g2i_ref, ...), custom_call_target="tpu_custom_call" | custom-call | flops 805306368 | tf_op jit(solution)/shard_map/pallas_call | solution.py:501
  37.0 3.2 %collective-permute-done.14 = f32[128,512]{1,0:T(8,128)S(1)} collective-permute-done((f32[128,512]{1,0:T(8,128)S(1)}, f32[128,512]{1,0:T(8,128)S(1)}, u32[]{:S(2)}, u32[]{:S(2)}) %collective-permute-start.14) | collective-permute-done | bytes 262176 | tf_op jit(solution)/shard_map/ppermute | solution.py:521
  40.2 1.7 %collective-permute-done.12 = f32[128,512]{1,0:T(8,128)S(1)} collective-permute-done((f32[128,512]{1,0:T(8,128)S(1)}, f32[128,512]{1,0:T(8,128)S(1)}, u32[]{:S(2)}, u32[]{:S(2)}) %collective-permute-start.12) | collective-permute-done | bytes 262176 | tf_op jit(solution)/shard_map/ppermute | solution.py:521
  43.8 2.5 %shard_map.166.parts_ref = f32[8,512]{1,0:T(8,128)S(1)} custom-call(f32[3,1,512]{2,1,0:T(1,128)S(1)} %bitcast.7, bf16[1,512,512]{2,1,0:T(8,128)(2,1)S(1)} %copy-done.1, f32[256,128]{1,0:T(8,128)S(1)} %get-tuple-element.62.si_ref, f32[256,128]{1,0:T(8,128)S(1)} %get-tuple-element.63.ti_ref, f32[256,512]{1,0:T(8,128)S(1)} %get-tuple-element.64.a0i_ref, ...), custom_call_target="tpu_custom_call" | custom-call | flops 805306368 | tf_op jit(solution)/shard_map/pallas_call | solution.py:501
  46.2 1.9 %collective-permute-done.15 = f32[64,512]{1,0:T(8,128)S(1)} collective-permute-done((f32[64,512]{1,0:T(8,128)S(1)}, f32[64,512]{1,0:T(8,128)S(1)}, u32[]{:S(2)}, u32[]{:S(2)}) %collective-permute-start.15) | collective-permute-done | bytes 131104 | tf_op jit(solution)/shard_map/ppermute | solution.py:521
  48.1 3.6 %collective-permute-start.16 = (f32[64,512]{1,0:T(8,128)S(1)}, f32[64,512]{1,0:T(8,128)S(1)}, u32[]{:S(2)}, u32[]{:S(2)}) collective-permute-start(f32[64,512]{1,0:T(8,128)S(1)} %add.75), channel_id=1, source_target_pairs={{0,4},{1,5},{2,6},{3,7},{4,0},{5,1},{6,2},{7,3},{8,12},{9,13},{10,... | collective-permute-start | bytes 393224 | tf_op jit(solution)/shard_map/ppermute | solution.py:521
  51.7 3.8 %collective-permute-done.16 = f32[64,512]{1,0:T(8,128)S(1)} collective-permute-done((f32[64,512]{1,0:T(8,128)S(1)}, f32[64,512]{1,0:T(8,128)S(1)}, u32[]{:S(2)}, u32[]{:S(2)}) %collective-permute-start.16) | collective-permute-done | bytes 131104 | tf_op jit(solution)/shard_map/ppermute | solution.py:521
  57.0 2.0 %collective-permute-start.19 = (f32[64,512]{1,0:T(8,128)S(1)}, f32[64,512]{1,0:T(8,128)S(1)}, u32[]{:S(2)}, u32[]{:S(2)}) collective-permute-start(f32[64,512]{1,0:T(8,128)S(1)} %add.76.refs_0_), channel_id=1, source_target_pairs={{0,24},{8,16},{16,8},{24,0},{1,25},{9,17},{17,9},{25,1},{2,26},{10... | collective-permute-start | bytes 393224 | tf_op jit(solution)/shard_map/ppermute | solution.py:521
  59.1 2.1 %shard_map.167 = (f32[3,1,512]{2,1,0:T(1,128)}, f32[1,512,512]{2,1,0:T(8,128)}, f32[1,512]{1,0:T(1,128)}, f32[1,512]{1,0:T(1,128)}, f32[1,512]{1,0:T(1,128)}, /*index=5*/f32[1,1]{1,0:T(1,128)}) custom-call(f32[8,512]{1,0:T(8,128)S(1)} %add.65.sums_ref, f32[8,512]{1,0:T(8,128)S(1)} %shard_map.166.parts_ref, f32[8,512]{1,0:T(8,128)S(1)} %get-tuple-element.50.isums_ref, ...), custom_call_target="tpu_custom_call" | custom-call | flops 939524096 | tf_op jit(solution)/shard_map/pallas_call | solution.py:501
  61.4 1.5 %collective-permute-done.19.refs_3_ = f32[64,512]{1,0:T(8,128)S(1)} collective-permute-done((f32[64,512]{1,0:T(8,128)S(1)}, f32[64,512]{1,0:T(8,128)S(1)}, u32[]{:S(2)}, u32[]{:S(2)}) %collective-permute-start.19) | collective-permute-done | bytes 131104 | tf_op jit(solution)/shard_map/ppermute | solution.py:521
  65.0 1.0 %shard_map.168 = f32[1,512,512]{2,1,0:T(8,128)} custom-call(f32[64,512]{1,0:T(8,128)S(1)} %add.76.refs_0_, f32[64,512]{1,0:T(8,128)S(1)} %collective-permute-done.17.refs_1_, f32[64,512]{1,0:T(8,128)S(1)} %collective-permute-done.18.refs_2_, f32[64,512]{1,0:T(8,128)S(1)} %collective-permute-done.19.refs_3_, f32[64,512]{1,0:T(8,128)S(1)} %collective-permute-done.20.refs_4_, ...), custom_call_target="tpu_custom_call" | custom-call | flops 262144 | tf_op jit(solution)/shard_map/pallas_call | solution.py:501
  (72 shorter events, 9.6 us)
Async XLA Ops:
  3.7 13.3 %collective-permute-start.1 = (f32[1,128]{1,0:T(1,128)S(1)}, f32[1,128]{1,0:T(1,128)S(1)}, u32[]{:S(2)}, u32[]{:S(2)}) collective-permute-start(f32[1,128]{1,0:T(1,128)S(1)} %get-tuple-element.95), channel_id=1, source_target_pairs={{0,8},{8,0},{16,24},{24,16},{1,9},{9,1},{17,25},{25,17},{2,10},{10... | collective-permute-start | bytes 1544 | tf_op jit(solution)/shard_map/ppermute | solution.py:536
  6.7 10.2 %collective-permute-start = (f32[1,128]{1,0:T(1,128)S(1)}, f32[1,128]{1,0:T(1,128)S(1)}, u32[]{:S(2)}, u32[]{:S(2)}) collective-permute-start(f32[1,128]{1,0:T(1,128)S(1)} %get-tuple-element.94), channel_id=1, source_target_pairs={{8,16},{16,8},{24,0},{0,24},{9,17},{17,9},{25,1},{1,25},{10,18},{1... | collective-permute-start | bytes 1544 | tf_op jit(solution)/shard_map/ppermute | solution.py:535
  8.2 8.8 %collective-permute-start.3 = (f32[1,128]{1,0:T(1,128)S(1)}, f32[1,128]{1,0:T(1,128)S(1)}, u32[]{:S(2)}, u32[]{:S(2)}) collective-permute-start(f32[1,128]{1,0:T(1,128)S(1)} %get-tuple-element.93), channel_id=1, source_target_pairs={{0,1},{1,0},{2,3},{3,2},{4,5},{5,4},{6,7},{7,6},{8,9},{9,8},{10,11... | collective-permute-start | bytes 1544 | tf_op jit(solution)/shard_map/ppermute | solution.py:536
  8.2 8.8 %collective-permute-start.2 = (f32[1,128]{1,0:T(1,128)S(1)}, f32[1,128]{1,0:T(1,128)S(1)}, u32[]{:S(2)}, u32[]{:S(2)}) collective-permute-start(f32[1,128]{1,0:T(1,128)S(1)} %get-tuple-element.96), channel_id=1, source_target_pairs={{1,2},{2,1},{3,4},{4,3},{5,6},{6,5},{7,0},{0,7},{9,10},{10,9},{11,... | collective-permute-start | bytes 1544 | tf_op jit(solution)/shard_map/ppermute | solution.py:535
  16.9 13.8 %collective-permute-start.10 = (f32[256,512]{1,0:T(8,128)S(1)}, f32[256,512]{1,0:T(8,128)S(1)}, u32[]{:S(2)}, u32[]{:S(2)}) collective-permute-start(f32[256,512]{1,0:T(8,128)S(1)} %slice.67), channel_id=1, source_target_pairs={{0,1},{1,0},{2,3},{3,2},{4,5},{5,4},{6,7},{7,6},{8,9},{9,8},{10,11... | collective-permute-start | bytes 1572872 | tf_op jit(solution)/shard_map/ppermute | solution.py:521
  18.4 1.4 %collective-permute-start.4 = (f32[8,512]{1,0:T(8,128)S(1)}, f32[8,512]{1,0:T(8,128)S(1)}, u32[]{:S(2)}, u32[]{:S(2)}) collective-permute-start(f32[8,512]{1,0:T(8,128)S(1)} %get-tuple-element.51), channel_id=1, source_target_pairs={{0,1},{1,0},{2,3},{3,2},{4,5},{5,4},{6,7},{7,6},{8,9},{9,8},{10,11... | collective-permute-start | bytes 49160 | tf_op jit(solution)/shard_map/ppermute | solution.py:521
  19.8 4.6 %collective-permute-start.7 = (f32[8,512]{1,0:T(8,128)S(1)}, f32[8,512]{1,0:T(8,128)S(1)}, u32[]{:S(2)}, u32[]{:S(2)}) collective-permute-start(f32[8,512]{1,0:T(8,128)S(1)} %add.60), channel_id=1, source_target_pairs={{0,24},{8,16},{16,8},{24,0},{1,25},{9,17},{17,9},{25,1},{2,26},{10... | collective-permute-start | bytes 49160 | tf_op jit(solution)/shard_map/ppermute | solution.py:521
  21.3 3.7 %collective-permute-start.6 = (f32[8,512]{1,0:T(8,128)S(1)}, f32[8,512]{1,0:T(8,128)S(1)}, u32[]{:S(2)}, u32[]{:S(2)}) collective-permute-start(f32[8,512]{1,0:T(8,128)S(1)} %add.60), channel_id=1, source_target_pairs={{0,16},{8,24},{16,0},{24,8},{1,17},{9,25},{17,1},{25,9},{2,18},{10... | collective-permute-start | bytes 49160 | tf_op jit(solution)/shard_map/ppermute | solution.py:521
  22.8 3.7 %collective-permute-start.5 = (f32[8,512]{1,0:T(8,128)S(1)}, f32[8,512]{1,0:T(8,128)S(1)}, u32[]{:S(2)}, u32[]{:S(2)}) collective-permute-start(f32[8,512]{1,0:T(8,128)S(1)} %add.60), channel_id=1, source_target_pairs={{0,8},{8,0},{16,24},{24,16},{1,9},{9,1},{17,25},{25,17},{2,10},{10... | collective-permute-start | bytes 49160 | tf_op jit(solution)/shard_map/ppermute | solution.py:521
  23.4 7.4 %collective-permute-start.11 = (f32[256,512]{1,0:T(8,128)S(1)}, f32[256,512]{1,0:T(8,128)S(1)}, u32[]{:S(2)}, u32[]{:S(2)}) collective-permute-start(f32[256,512]{1,0:T(8,128)S(1)} %slice.71), channel_id=1, source_target_pairs={{0,1},{1,0},{2,3},{3,2},{4,5},{5,4},{6,7},{7,6},{8,9},{9,8},{10,11... | collective-permute-start | bytes 1572872 | tf_op jit(solution)/shard_map/ppermute | solution.py:521
  26.5 3.7 %collective-permute-start.8 = (f32[8,512]{1,0:T(8,128)S(1)}, f32[8,512]{1,0:T(8,128)S(1)}, u32[]{:S(2)}, u32[]{:S(2)}) collective-permute-start(f32[8,512]{1,0:T(8,128)S(1)} %add_add_fusion.1), channel_id=1, source_target_pairs={{0,2},{1,3},{2,0},{3,1},{4,6},{5,7},{6,4},{7,5},{8,10},{9,11},{10,... | collective-permute-start | bytes 49160 | tf_op jit(solution)/shard_map/ppermute | solution.py:521
  30.3 6.7 %collective-permute-start.9 = (f32[8,512]{1,0:T(8,128)S(1)}, f32[8,512]{1,0:T(8,128)S(1)}, u32[]{:S(2)}, u32[]{:S(2)}) collective-permute-start(f32[8,512]{1,0:T(8,128)S(1)} %add.64), channel_id=1, source_target_pairs={{0,4},{1,5},{2,6},{3,7},{4,0},{5,1},{6,2},{7,3},{8,12},{9,13},{10,... | collective-permute-start | bytes 49160 | tf_op jit(solution)/shard_map/ppermute | solution.py:521
  31.0 9.3 %collective-permute-start.14 = (f32[128,512]{1,0:T(8,128)S(1)}, f32[128,512]{1,0:T(8,128)S(1)}, u32[]{:S(2)}, u32[]{:S(2)}) collective-permute-start(f32[128,512]{1,0:T(8,128)S(1)} %pad_maximum_fusion.2), channel_id=1, source_target_pairs={{0,24},{8,16},{16,8},{24,0},{1,25},{9,17},{17,9},{25,1},{2,26},{10... | collective-permute-start | bytes 786440 | tf_op jit(solution)/shard_map/ppermute | solution.py:521
  31.5 10.4 %collective-permute-start.12 = (f32[128,512]{1,0:T(8,128)S(1)}, f32[128,512]{1,0:T(8,128)S(1)}, u32[]{:S(2)}, u32[]{:S(2)}) collective-permute-start(f32[128,512]{1,0:T(8,128)S(1)} %pad_maximum_fusion), channel_id=1, source_target_pairs={{0,8},{8,0},{16,24},{24,16},{1,9},{9,1},{17,25},{25,17},{2,10},{10... | collective-permute-start | bytes 786440 | tf_op jit(solution)/shard_map/ppermute | solution.py:521
  33.1 9.8 %collective-permute-start.13 = (f32[128,512]{1,0:T(8,128)S(1)}, f32[128,512]{1,0:T(8,128)S(1)}, u32[]{:S(2)}, u32[]{:S(2)}) collective-permute-start(f32[128,512]{1,0:T(8,128)S(1)} %pad_maximum_fusion.1), channel_id=1, source_target_pairs={{0,16},{8,24},{16,0},{24,8},{1,17},{9,25},{17,1},{25,9},{2,18},{10... | collective-permute-start | bytes 786440 | tf_op jit(solution)/shard_map/ppermute | solution.py:521
  43.0 5.0 %collective-permute-start.15 = (f32[64,512]{1,0:T(8,128)S(1)}, f32[64,512]{1,0:T(8,128)S(1)}, u32[]{:S(2)}, u32[]{:S(2)}) collective-permute-start(f32[64,512]{1,0:T(8,128)S(1)} %fusion.1), channel_id=1, source_target_pairs={{0,2},{1,3},{2,0},{3,1},{4,6},{5,7},{6,4},{7,5},{8,10},{9,11},{10,... | collective-permute-start | bytes 393224 | tf_op jit(solution)/shard_map/ppermute | solution.py:521
  48.1 7.4 %collective-permute-start.16 = (f32[64,512]{1,0:T(8,128)S(1)}, f32[64,512]{1,0:T(8,128)S(1)}, u32[]{:S(2)}, u32[]{:S(2)}) collective-permute-start(f32[64,512]{1,0:T(8,128)S(1)} %add.75), channel_id=1, source_target_pairs={{0,4},{1,5},{2,6},{3,7},{4,0},{5,1},{6,2},{7,3},{8,12},{9,13},{10,... | collective-permute-start | bytes 393224 | tf_op jit(solution)/shard_map/ppermute | solution.py:521
  55.5 5.7 %collective-permute-start.17 = (f32[64,512]{1,0:T(8,128)S(1)}, f32[64,512]{1,0:T(8,128)S(1)}, u32[]{:S(2)}, u32[]{:S(2)}) collective-permute-start(f32[64,512]{1,0:T(8,128)S(1)} %add.76.refs_0_), channel_id=1, source_target_pairs={{0,8},{8,0},{16,24},{24,16},{1,9},{9,1},{17,25},{25,17},{2,10},{10... | collective-permute-start | bytes 393224 | tf_op jit(solution)/shard_map/ppermute | solution.py:521
  56.4 5.0 %collective-permute-start.18 = (f32[64,512]{1,0:T(8,128)S(1)}, f32[64,512]{1,0:T(8,128)S(1)}, u32[]{:S(2)}, u32[]{:S(2)}) collective-permute-start(f32[64,512]{1,0:T(8,128)S(1)} %add.76.refs_0_), channel_id=1, source_target_pairs={{0,16},{8,24},{16,0},{24,8},{1,17},{9,25},{17,1},{25,9},{2,18},{10... | collective-permute-start | bytes 393224 | tf_op jit(solution)/shard_map/ppermute | solution.py:521
  57.0 5.9 %collective-permute-start.19 = (f32[64,512]{1,0:T(8,128)S(1)}, f32[64,512]{1,0:T(8,128)S(1)}, u32[]{:S(2)}, u32[]{:S(2)}) collective-permute-start(f32[64,512]{1,0:T(8,128)S(1)} %add.76.refs_0_), channel_id=1, source_target_pairs={{0,24},{8,16},{16,8},{24,0},{1,25},{9,17},{17,9},{25,1},{2,26},{10... | collective-permute-start | bytes 393224 | tf_op jit(solution)/shard_map/ppermute | solution.py:521
  62.9 1.3 %collective-permute-start.20 = (f32[64,512]{1,0:T(8,128)S(1)}, f32[64,512]{1,0:T(8,128)S(1)}, u32[]{:S(2)}, u32[]{:S(2)}) collective-permute-start(f32[64,512]{1,0:T(8,128)S(1)} %add.76.refs_0_), channel_id=1, source_target_pairs={{0,1},{1,0},{2,3},{3,2},{4,5},{5,4},{6,7},{7,6},{8,9},{9,8},{10,11... | collective-permute-start | bytes 393224 | tf_op jit(solution)/shard_map/ppermute | solution.py:521
  62.9 1.5 %collective-permute-start.21 = (f32[64,512]{1,0:T(8,128)S(1)}, f32[64,512]{1,0:T(8,128)S(1)}, u32[]{:S(2)}, u32[]{:S(2)}) collective-permute-start(f32[64,512]{1,0:T(8,128)S(1)} %collective-permute-done.17.refs_1_), channel_id=1, source_target_pairs={{0,1},{1,0},{2,3},{3,2},{4,5},{5,4},{6,7},{7,6},{8,9},{9,8},{10,11... | collective-permute-start | bytes 393224 | tf_op jit(solution)/shard_map/ppermute | solution.py:521
  63.4 1.3 %collective-permute-start.22 = (f32[64,512]{1,0:T(8,128)S(1)}, f32[64,512]{1,0:T(8,128)S(1)}, u32[]{:S(2)}, u32[]{:S(2)}) collective-permute-start(f32[64,512]{1,0:T(8,128)S(1)} %collective-permute-done.18.refs_2_), channel_id=1, source_target_pairs={{0,1},{1,0},{2,3},{3,2},{4,5},{5,4},{6,7},{7,6},{8,9},{9,8},{10,11... | collective-permute-start | bytes 393224 | tf_op jit(solution)/shard_map/ppermute | solution.py:521
  63.4 1.5 %collective-permute-start.23 = (f32[64,512]{1,0:T(8,128)S(1)}, f32[64,512]{1,0:T(8,128)S(1)}, u32[]{:S(2)}, u32[]{:S(2)}) collective-permute-start(f32[64,512]{1,0:T(8,128)S(1)} %collective-permute-done.19.refs_3_), channel_id=1, source_target_pairs={{0,1},{1,0},{2,3},{3,2},{4,5},{5,4},{6,7},{7,6},{8,9},{9,8},{10,11... | collective-permute-start | bytes 393224 | tf_op jit(solution)/shard_map/ppermute | solution.py:521
  (10 other events, 107.7 us)
